TPU v7x, 32 devices: a whole 2x2x4 slice. The times are simulated.
32 devices in a mesh: gx: 4 (over z), gy: 4 (over y, x), gz: 2 (over core).
Axes of the slice: x: 2, y: 2, z: 4, core: 2. Of those that a mesh axis runs over, the one named last changes fastest.
Arguments:
- positions: float32 [3, 64, 64, 512], P(None, 'gx', 'gy', 'gz'), may hold values from -6 to 6
- pair_node: int32 [4, 4, 2, 32, 256], P('gx', 'gy', 'gz'), may hold values from 0 to 255
- pair_line: int32 [4, 4, 2, 32], P('gx', 'gy', 'gz'), may hold values from 0 to 255
- pair_far: int32 [4, 4, 2, 32, 256], P('gx', 'gy', 'gz'), may hold values from 0 to 261, as said below
- far_line: int32 [4, 4, 2, 32], P('gx', 'gy', 'gz'), may hold values from 0 to 483, as said below
- pair_geom: float32 [4, 4, 2, 32, 4, 256], P('gx', 'gy', 'gz'), may hold values from -4 to 4
- live_blocks: int32 [4, 4, 2], P('gx', 'gy', 'gz'), may hold values from 8 to 32, as said below
Outputs:
- corrected: float32 [3, 64, 64, 512], P(None, 'gx', 'gy', 'gz')
- sweep_history: float32 [2, 5], replicated
Inputs may be any that keep to these rules, and one draw needn't show every extreme that they name: `pair_far`: together with far_line: at most one of the three coordinates of node b lies outside the owner block's own nodes; node b lies inside the whole grid; in slots below 16 node b is one of the owner block's own nodes. `far_line`: together with pair_far, as stated there. `live_blocks`: some owner block has all 32 slots live.
All inputs are finite; a program needn't handle non-finite values.
Results may differ from a plain program's by a relative error of at most 0.0001.
Values sent between devices are 32-bit elements; how exact they have to be, the bound alone decides.
A program may use at most 64 MiB of HBM per device.

v0:
```python
import functools

import jax
import jax.numpy as jnp
from jax import lax
from jax.experimental import pallas as pl
from jax.experimental.pallas import tpu as pltpu
from jax.sharding import PartitionSpec as P

RIM = 3
SWEEPS = 5
RELAX = 0.9
AXES = ("gx", "gy", "gz")
MESH = pl.DeviceIdType.MESH
f32 = jnp.float32
bf16 = jnp.bfloat16


def split(x, parts):
    out = []
    for _ in range(parts - 1):
        hi = x.astype(bf16)
        out.append(hi)
        x = x - hi.astype(f32)
    out.append(x.astype(bf16))
    return out


def mm(a, b):
    return jnp.dot(a, b, preferred_element_type=f32)


def take_lanes(x, low, half):
    outs = []
    for h in range(0, low.shape[1], 128):
        idx = low[:, h : h + 128]
        got = jnp.take_along_axis(x[:, :128], idx, axis=1, mode="promise_in_bounds")
        for j in range(1, x.shape[1] // 128):
            more = jnp.take_along_axis(
                x[:, 128 * j : 128 * (j + 1)], idx, axis=1, mode="promise_in_bounds"
            )
            got = jnp.where(half[:, h : h + 128] == j, more, got)
        outs.append(got)
    return jnp.concatenate(outs, axis=1)


def kernel(
    sizes,
    blk,
    live_ref,
    node_ref,
    line_ref,
    farpos_ref,
    farline_ref,
    geom_ref,
    pos_hbm,
    acc_ref,
    hist_ref,
    pos_ref,
    req,
    cols,
    hot,
    two,
    amat,
    cinv,
    geo,
    low_ref,
    half_ref,
    gap,
    wcat,
    reqs,
    dsend,
    drecv,
    erecv,
    rrecv,
    pos_sem,
    qs_sem,
    qr_sem,
    ds_sem,
    dr_sem,
    es_sem,
    er_sem,
    rs_sem,
    rr_sem,
):
    nx, ny, nz = sizes
    bx, by, bz = blk
    devices = nx * ny * nz
    blocks, pairs = gap.shape
    outer = blocks // 2
    lines = bx * by
    me = [lax.axis_index(a) for a in AXES]
    mine = (me[0] * ny + me[1]) * nz + me[2]
    dirs = [(a, s) for a in (1, 0, 2) for s in (1, -1)]

    def neighbour(axis, sign):
        to = list(me)
        to[axis] = lax.rem(me[axis] + sign + sizes[axis], sizes[axis])
        return tuple(to)

    def exists(axis, sign):
        return (me[axis] + sign >= 0) & (me[axis] + sign < sizes[axis])

    def coords(k):
        to = lax.rem(mine + k, devices)
        return (to // (ny * nz), lax.rem(to // nz, ny), lax.rem(to, nz))

    pos_copy = pltpu.make_async_copy(pos_hbm, pos_ref, pos_sem)
    pos_copy.start()

    def column(ref):
        row = ref[0, 0].astype(f32)
        return jnp.transpose(jnp.broadcast_to(row, (pairs, blocks)))

    wide = pairs // 128
    planes = [geom_ref[0, 0, 0, outer:, c, :] for c in range(3)]
    planes.append(farpos_ref[0, 0, 0, outer:, :].astype(f32))
    for c in range(4):
        for h in range(wide):
            req[c * wide + h] = planes[c][:, 128 * h : 128 * (h + 1)]
    cols[1] = column(farline_ref)
    req[4 * wide] = cols[1, outer:, :128]
    cols[0] = column(line_ref)
    def ask(d, axis, sign):
        return pltpu.make_async_remote_copy(
            src_ref=req,
            dst_ref=reqs.at[d],
            send_sem=qs_sem.at[d],
            recv_sem=qr_sem.at[d],
            device_id=neighbour(axis, sign),
            device_id_type=MESH,
        )

    for d, (axis, sign) in enumerate(dirs):

        @pl.when(exists(axis, sign))
        def _():
            ask(d, axis, sign).start()

    for d, (axis, sign) in enumerate(dirs):

        @pl.when(jnp.logical_not(exists(axis, -sign)))
        def _():
            reqs[d] = jnp.zeros(req.shape, f32)

        @pl.when(jnp.logical_not(exists(axis, sign)))
        def _():
            for t in range(SWEEPS):
                drecv[t, d] = jnp.zeros((outer, pairs), f32)

    live = jnp.broadcast_to(live_ref[0], (blocks, pairs))
    live_rows = lax.broadcasted_iota(jnp.int32, (blocks, pairs), 0) < live
    lane_node = lax.broadcasted_iota(jnp.int32, (pairs, bz), 1).astype(f32)
    node_t = jnp.transpose(node_ref[0, 0, 0].astype(f32))
    for b in range(blocks):
        hot[pl.ds(b * pairs, pairs), :] = jnp.where(
            node_t[:, b : b + 1] == lane_node, 1.0, 0.0
        ).astype(bf16)
    row_line = line_ref[0, 0].astype(f32)
    two[...] = jnp.concatenate([row_line, row_line], axis=1)
    row_mod = lax.broadcasted_iota(jnp.int32, (blocks, blocks), 0)
    col_mod = lax.broadcasted_iota(jnp.int32, (blocks, blocks), 1)
    line_b = cols[0]
    same = line_b[:, :blocks] == row_line
    first_col = 1.0 - jnp.max(
        jnp.where(same & (col_mod < row_mod), 1.0, 0.0), axis=1, keepdims=True
    )

    def expand(stack, step):
        rows = stack.shape[0]
        which = lax.rem(lax.broadcasted_iota(jnp.int32, (rows, pairs), 0), step)
        return jnp.concatenate(
            [jnp.where(which == j, stack, 0.0).astype(bf16) for j in range(step)], axis=1
        )

    counts = []
    for g in range(blocks // 8):
        ones = jnp.where(live_rows[8 * g : 8 * g + 8], 1.0, 0.0)
        counts.append(mm(expand(ones, 8), hot[pl.ds(8 * g * pairs, 8 * pairs), :]))
    counts = jnp.concatenate(counts, axis=0).astype(bf16)

    def located(code, zpos, shift):
        e = jnp.floor((code + 0.5) / (by + 2 * RIM))
        f = code - e * (by + 2 * RIM)
        e = e - (RIM + shift[0] * bx)
        f = f - (RIM + shift[1] * by)
        z = zpos - (RIM + shift[2] * bz)
        ok_line = (e >= 0) & (e < bx) & (f >= 0) & (f < by)
        return jnp.where(ok_line, e * by + f, -1.0), z, ok_line & (z >= 0) & (z < bz)

    def setup(row, line, node, geom):
        n = line.shape[0]
        lane_line = lax.broadcasted_iota(jnp.int32, (n, lines), 1).astype(f32)
        a = jnp.where(line[:, : 2 * blocks] == two[...], 1.0, 0.0).astype(bf16)
        amat[pl.ds(row, n), :] = a
        cinv[pl.ds(row, n), :] = RELAX / (1.0 + mm(a[:, :blocks], counts))
        idx = node.astype(jnp.int32)
        low = lax.bitwise_and(idx, 127)
        half = lax.shift_right_logical(idx, 7)
        low_ref[pl.ds(row, n), :] = low
        half_ref[pl.ds(row, n), :] = half
        own = jnp.where(line == lane_line, 1.0, 0.0).astype(bf16)
        total = jnp.zeros((n, pairs), f32)
        for c in range(3):
            geo[c, pl.ds(row, n), :] = geom[c]
            vals = jnp.zeros((n, bz), f32)
            for part in split(pos_ref[c].reshape(lines, bz), 3):
                vals += mm(own, part)
            total += geom[c] * take_lanes(vals, low, half)
        return total

    def cat(parts):
        return jnp.concatenate(parts, axis=0)

    pos_copy.wait()
    for d, (axis, sign) in enumerate(dirs):

        @pl.when(exists(axis, -sign))
        def _():
            ask(d, axis, sign).wait_recv()

    asked = []
    for d, (axis, sign) in enumerate(dirs):
        shift = [0, 0, 0]
        shift[axis] = sign
        got = [
            jnp.concatenate([reqs[d, c * wide + h] for h in range(wide)], axis=1) for c in range(4)
        ]
        code = jnp.concatenate([reqs[d, 4 * wide]] * wide, axis=1)
        line, z, ok = located(code, got[3], shift)
        asked.append(
            [line, jnp.where(ok, z, 0.0)] + [jnp.where(ok, -got[c], 0.0) for c in range(3)]
        )
    asked = [cat([x[i] for x in asked]) for i in range(5)]
    base = asked[0].shape[0]
    rows = base + 2 * blocks

    def respond(t, total):
        for d, (axis, sign) in enumerate(dirs):
            dsend[t, d] = total[d * outer : (d + 1) * outer]
        for d, (axis, sign) in enumerate(dirs):

            @pl.when(exists(axis, -sign))
            def _():
                answer(t, d, axis, sign).start()

    def answer(t, d, axis, sign):
        return pltpu.make_async_remote_copy(
            src_ref=dsend.at[t, d],
            dst_ref=drecv.at[t, d],
            send_sem=ds_sem.at[t, d],
            recv_sem=dr_sem.at[t, d],
            device_id=neighbour(axis, -sign),
            device_id_type=MESH,
        )

    def received(t):
        for d, (axis, sign) in enumerate(dirs):

            @pl.when(exists(axis, sign))
            def _():
                answer(t, d, axis, sign).wait_recv()

        got = drecv[t, 0]
        for d in range(1, len(dirs)):
            got = got + drecv[t, d]
        return got

    respond(0, setup(0, asked[0], asked[1], asked[2:]))

    line, z, ok = located(cols[1], farpos_ref[0, 0, 0].astype(f32), (0, 0, 0))
    geom = [geom_ref[0, 0, 0, :, c, :] for c in range(4)]
    start = setup(
        base,
        cat([line_b, line]),
        cat([node_ref[0, 0, 0].astype(f32), jnp.where(ok, z, 0.0)]),
        [cat([geom[c], jnp.where(ok, -geom[c], 0.0)]) for c in range(3)],
    )
    start = start[:blocks] + start[blocks:] - geom[3]
    gap[0:outer, :] = start[:outer]
    gap[pl.ds(outer, outer), :] = start[outer:] + received(0)
    acc_ref[...] = jnp.zeros_like(acc_ref)

    def to_all(ref, send_sem, recv_sem):
        def send(k, carry):
            pltpu.make_async_remote_copy(
                src_ref=ref,
                dst_ref=ref,
                send_sem=send_sem,
                recv_sem=recv_sem,
                device_id=coords(k),
                device_id_type=MESH,
            ).start()
            return carry

        lax.fori_loop(1, devices, send, 0, unroll=devices <= 32)

    def lanes_sum(x):
        x = jnp.sum(x, axis=0, keepdims=True)
        out = x[:, :128]
        for j in range(1, x.shape[1] // 128):
            out = out + x[:, 128 * j : 128 * (j + 1)]
        return out

    lane = lax.broadcasted_iota(jnp.int32, (1, 128), 1)

    def apply(row, n, parts):
        both = mm(amat[row : row + n, :], parts)
        return [both[:, c * bz : (c + 1) * bz] * cinv[row : row + n, :] for c in range(3)]

    def dots(row, n, moved):
        low = low_ref[row : row + n, :]
        half = half_ref[row : row + n, :]
        total = geo[0, row : row + n] * take_lanes(moved[0], low, half)
        for c in range(1, 3):
            total += geo[c, row : row + n] * take_lanes(moved[c], low, half)
        return total

    def sweep(t, last):
        depth = jnp.where(live_rows, jnp.maximum(-gap[...], 0.0), 0.0)
        squares = lanes_sum(depth * depth)
        if not last:
            erecv[t, mine] = squares
            to_all(erecv.at[t, mine], es_sem.at[t], er_sem.at[t])
        for g in range(blocks // 8):
            lo, hi = 8 * g, 8 * g + 8
            terms = cat([depth[lo:hi] * geo[c, base + lo : base + hi] for c in range(3)])
            top = terms.astype(bf16).astype(f32)
            sums = mm(expand(cat([top, terms - top]), 8), hot[pl.ds(lo * pairs, 8 * pairs), :])
            sums = sums[:24] + sums[24:]
            for c in range(3):
                wcat[lo:hi, c * bz : (c + 1) * bz] = sums[8 * c : 8 * c + 8]
        parts = cat(split(wcat[...], 2))
        if not last:
            respond(t + 1, dots(0, base, apply(0, base, parts)))
        moved = apply(base, blocks if last else 2 * blocks, parts)
        near = jnp.concatenate([m[:blocks] for m in moved], axis=1)
        resid = jnp.sum(lanes_sum(near * near * first_col), axis=1, keepdims=True)
        rrecv[mine] = jnp.where(lane == t, resid, rrecv[mine])
        if last:
            energy = jnp.sum(squares, axis=1, keepdims=True)
            rrecv[mine] = jnp.where(lane == SWEEPS, energy, rrecv[mine])
            to_all(rrecv.at[mine], rs_sem, rr_sem)
            others = rrecv.at[pl.ds(0, devices - 1)]
            pltpu.make_async_copy(others, others, rr_sem).wait()
            energy = jnp.sum(rrecv[...], axis=0)[:, SWEEPS : SWEEPS + 1]
        else:
            step = dots(base, 2 * blocks, moved)
            step = step[:blocks] + step[blocks:]
            others = erecv.at[t, pl.ds(0, devices - 1)]
            pltpu.make_async_copy(others, others, er_sem.at[t]).wait()
            energy = jnp.sum(jnp.sum(erecv[t], axis=0), axis=1, keepdims=True)
        scale = 1.0 / (1.0 + energy / (blocks * pairs * devices))
        hist_ref[0:1, :] = jnp.where(lane == t, energy, hist_ref[0:1, :])
        hist_ref[1:2, :] = jnp.where(lane == t, scale, hist_ref[1:2, :])
        acc_ref[...] = acc_ref[...] + (scale * first_col) * near
        if not last:
            more = received(t + 1)
            gap[0:outer, :] = gap[0:outer, :] + scale * step[:outer]
            gap[pl.ds(outer, outer), :] = gap[pl.ds(outer, outer), :] + scale * (
                step[outer:] + more
            )

    rrecv[mine] = jnp.zeros((1, 128), f32)
    hist_ref[...] = jnp.zeros_like(hist_ref)

    def body(t, carry):
        sweep(t, False)
        return carry

    lax.fori_loop(0, SWEEPS - 1, body, 0)
    sweep(SWEEPS - 1, True)

    for d, (axis, sign) in enumerate(dirs):

        @pl.when(exists(axis, sign))
        def _():
            ask(d, axis, sign).wait_send()

        @pl.when(exists(axis, -sign))
        def _():
            for t in range(SWEEPS):
                answer(t, d, axis, sign).wait_send()

    for t in range(SWEEPS - 1):
        ref = erecv.at[t, pl.ds(0, devices - 1)]
        pltpu.make_async_copy(ref, ref, es_sem.at[t]).wait()
    others = rrecv.at[pl.ds(0, devices - 1)]
    pltpu.make_async_copy(others, others, rs_sem).wait()
    energy, scale = hist_ref[0:1, :], hist_ref[1:2, :]
    resid = jnp.sum(rrecv[...], axis=0)
    hist_ref[0:1, :] = jnp.sqrt(1.0 + energy / (blocks * pairs))
    hist_ref[1:2, :] = jnp.sqrt(1.0 + scale * scale * resid / (bx * by * bz))


def finish(acc_ref, line_ref, hist_in, pos_ref, out_ref, hist_ref):
    _, bx, by, bz = pos_ref.shape
    lines = bx * by
    row = line_ref[0, 0].astype(f32)
    row = jnp.concatenate([row, row], axis=1)
    rows = lax.broadcasted_iota(jnp.int32, (lines, row.shape[1]), 0).astype(f32)
    place = jnp.where(rows == row, 1.0, 0.0).astype(bf16)
    total = mm(place, jnp.concatenate(split(acc_ref[...], 2), axis=0))
    out_ref[0] = pos_ref[0] + total.reshape(bx, by, bz)
    hist_ref[...] = hist_in[0:2, : hist_ref.shape[1]]


def local(sizes, positions, pair_node, pair_line, pair_far, far_line, pair_geom, live_blocks):
    blocks, pairs = pair_node.shape[3:]
    blk = positions.shape[1:]
    devices = sizes[0] * sizes[1] * sizes[2]
    outer = blocks // 2
    rows = 2 * blocks + 6 * outer
    dma = pltpu.SemaphoreType.DMA
    vmem = pl.BlockSpec(memory_space=pltpu.VMEM)
    moved, hist = pl.pallas_call(
        functools.partial(kernel, sizes, blk),
        out_shape=(
            jax.ShapeDtypeStruct((blocks, 3 * blk[2]), f32),
            jax.ShapeDtypeStruct((8, 128), f32),
        ),
        in_specs=[vmem] * 6 + [pl.BlockSpec(memory_space=pl.ANY)],
        out_specs=(vmem, vmem),
        scratch_shapes=[
            pltpu.VMEM(positions.shape, f32),
            pltpu.VMEM((4 * (pairs // 128) + 1, outer, 128), f32),
            pltpu.VMEM((2, blocks, pairs), f32),
            pltpu.VMEM((blocks * pairs, blk[2]), bf16),
            pltpu.VMEM((1, 2 * blocks), f32),
            pltpu.VMEM((rows, 2 * blocks), bf16),
            pltpu.VMEM((rows, pairs), f32),
            pltpu.VMEM((3, rows, pairs), f32),
            pltpu.VMEM((rows, pairs), jnp.int32),
            pltpu.VMEM((rows, pairs), jnp.int32),
            pltpu.VMEM((blocks, pairs), f32),
            pltpu.VMEM((blocks, 3 * blk[2]), f32),
            pltpu.VMEM((6, 4 * (pairs // 128) + 1, outer, 128), f32),
            pltpu.VMEM((SWEEPS, 6, outer, pairs), f32),
            pltpu.VMEM((SWEEPS, 6, outer, pairs), f32),
            pltpu.VMEM((SWEEPS, devices, 1, 128), f32),
            pltpu.VMEM((devices, 1, 128), f32),
            dma,
            dma((6,)),
            dma((6,)),
            dma((SWEEPS, 6)),
            dma((SWEEPS, 6)),
            dma((SWEEPS,)),
            dma((SWEEPS,)),
            dma,
            dma,
        ],
        compiler_params=pltpu.CompilerParams(has_side_effects=True),
    )(live_blocks, pair_node, pair_line, pair_far, far_line, pair_geom, positions)
    return pl.pallas_call(
        finish,
        grid=(3,),
        out_shape=(
            jax.ShapeDtypeStruct(positions.shape, f32),
            jax.ShapeDtypeStruct((2, SWEEPS), f32),
        ),
        in_specs=[
            pl.BlockSpec((blocks, blk[2]), lambda c: (0, c)),
            pl.BlockSpec(pair_line.shape, lambda c: (0, 0, 0, 0)),
            pl.BlockSpec((8, 128), lambda c: (0, 0)),
            pl.BlockSpec((1,) + blk, lambda c: (c, 0, 0, 0)),
        ],
        out_specs=(
            pl.BlockSpec((1,) + blk, lambda c: (c, 0, 0, 0)),
            pl.BlockSpec((2, SWEEPS), lambda c: (0, 0)),
        ),
    )(moved, pair_line, hist, positions)


def solution(mesh):
    sizes = tuple(mesh.shape[a] for a in AXES)
    return jax.shard_map(
        functools.partial(local, sizes),
        mesh=mesh,
        in_specs=(
            P(None, "gx", "gy", "gz"),
            P("gx", "gy", "gz", None, None),
            P("gx", "gy", "gz", None),
            P("gx", "gy", "gz", None, None),
            P("gx", "gy", "gz", None),
            P("gx", "gy", "gz", None, None, None),
            P("gx", "gy", "gz"),
        ),
        out_specs=(P(None, "gx", "gy", "gz"), P()),
        check_vma=False,
    )
```

profile of v0, /device:TPU:0, one launch (start us, length us, event | category | flops | bytes accessed | tf_op | source)
XLA Modules:
  0.0 52.0 jit_solution(6239819224979550876)
XLA Ops:
  1.3 47.5 %shard_map.86 = (f32[32,768]{1,0:T(8,128)}, f32[8,128]{1,0:T(8,128)}) custom-call(s32[1,1,1]{2,1,0:T(1,128)S(6)} %copy.9.live_ref, s32[1,1,1,32,256]{4,3,2,1,0:T(8,128)} %node_ref.1, s32[1,1,1,32]{3,2,1,0:T(1,128)} %line_ref.3, s32[1,1,1,32,256]{4,3,2,1,0:T(8,128)} %farpos_ref.1, s32[1,1,1,32]{3,2,1,0:T(1,128)} %farline_ref.1, ...), custom_call_target="tpu_custom_call" | custom-call | tf_op jit(solution)/shard_map/pallas_call | solution.py:416
  48.8 3.2 %shard_map.87 = (f32[3,16,16,256]{3,2,1,0:T(8,128)}, f32[2,5]{1,0:T(2,128)}) custom-call(f32[32,768]{1,0:T(8,128)} %get-tuple-element.4.acc_ref, s32[1,1,1,32]{3,2,1,0:T(1,128)} %line_ref.3, f32[8,128]{1,0:T(8,128)} %get-tuple-element.5.hist_in, f32[3,16,16,256]{3,2,1,0:T(8,128)} %pos_ref.1), custom_call_target="tpu_custom_call" | custom-call | tf_op jit(solution)/shard_map/pallas_call | solution.py:454
where the time goes:
time: 52.2 us; the launch traced here: 52 us
  Pallas kernels  50.7 us (97%)
  between operations  1.29 us (2%)
    pallas_call x1, Pallas kernels, local(): pl.pallas_call(functools.partial(kernel, sizes, blk), out_shape=(jax.Shap...  47.5 us
    pallas_call x1, Pallas kernels, local(): pl.pallas_call(finish, grid=(3,), out_shape=(jax.ShapeDtypeStruct(positio...  3.24 us

commit v1 on v0

--- a/solution.py
+++ b/solution.py
@@ -47,15 +47,21 @@
 def kernel(
     sizes,
     blk,
+    live_hbm,
+    node_hbm,
+    line_hbm,
+    farpos_hbm,
+    farline_hbm,
+    geom_hbm,
+    pos_hbm,
+    acc_ref,
+    hist_ref,
     live_ref,
     node_ref,
     line_ref,
     farpos_ref,
     farline_ref,
     geom_ref,
-    pos_hbm,
-    acc_ref,
-    hist_ref,
     pos_ref,
     req,
     cols,
@@ -73,7 +79,9 @@
     drecv,
     erecv,
     rrecv,
-    pos_sem,
+    in_sem,
+    plane_sem,
+    whole_sem,
     qs_sem,
     qr_sem,
     ds_sem,
@@ -105,8 +113,39 @@
         to = lax.rem(mine + k, devices)
         return (to // (ny * nz), lax.rem(to // nz, ny), lax.rem(to, nz))
 
-    pos_copy = pltpu.make_async_copy(pos_hbm, pos_ref, pos_sem)
-    pos_copy.start()
+    def moved_by(axis, k):
+        to = me[axis] + k
+        return jnp.where(to >= sizes[axis], to - sizes[axis], to) if k else to
+
+    ids = [[moved_by(a, k) for k in range(sizes[a])] for a in range(3)]
+
+    def signal_line(sem, axis):
+        for k in range(1, sizes[axis]):
+            to = list(me)
+            to[axis] = ids[axis][k]
+            pl.semaphore_signal(sem, inc=1, device_id=tuple(to), device_id_type=MESH)
+
+    barrier = pltpu.get_barrier_semaphore()
+    for axis in range(3):
+        signal_line(barrier, axis)
+    inputs = [
+        pltpu.make_async_copy(src, dst, in_sem.at[i])
+        for i, (src, dst) in enumerate(
+            [
+                (farline_hbm, farline_ref),
+                (farpos_hbm, farpos_ref),
+                (geom_hbm, geom_ref),
+                (node_hbm, node_ref),
+                (line_hbm, line_ref),
+                (live_hbm, live_ref),
+                (pos_hbm, pos_ref),
+            ]
+        )
+    ]
+    for copy in inputs:
+        copy.start()
+    for copy in inputs[:3]:
+        copy.wait()
 
     def column(ref):
         row = ref[0, 0].astype(f32)
@@ -120,7 +159,7 @@
             req[c * wide + h] = planes[c][:, 128 * h : 128 * (h + 1)]
     cols[1] = column(farline_ref)
     req[4 * wide] = cols[1, outer:, :128]
-    cols[0] = column(line_ref)
+
     def ask(d, axis, sign):
         return pltpu.make_async_remote_copy(
             src_ref=req,
@@ -131,11 +170,17 @@
             device_id_type=MESH,
         )
 
+    pl.semaphore_wait(barrier, sum(sizes) - 3)
     for d, (axis, sign) in enumerate(dirs):
 
         @pl.when(exists(axis, sign))
         def _():
             ask(d, axis, sign).start()
+
+    signal_line(plane_sem, 0)
+    for copy in inputs[3:6]:
+        copy.wait()
+    cols[0] = column(line_ref)
 
     for d, (axis, sign) in enumerate(dirs):
 
@@ -212,13 +257,16 @@
     def cat(parts):
         return jnp.concatenate(parts, axis=0)
 
-    pos_copy.wait()
+    inputs[6].wait()
     for d, (axis, sign) in enumerate(dirs):
 
         @pl.when(exists(axis, -sign))
         def _():
             ask(d, axis, sign).wait_recv()
 
+    if nx > 1:
+        pl.semaphore_wait(plane_sem, nx - 1)
+    signal_line(whole_sem, 2)
     asked = []
     for d, (axis, sign) in enumerate(dirs):
         shift = [0, 0, 0]
@@ -277,23 +325,36 @@
         [cat([geom[c], jnp.where(ok, -geom[c], 0.0)]) for c in range(3)],
     )
     start = start[:blocks] + start[blocks:] - geom[3]
+    if nz > 1:
+        pl.semaphore_wait(whole_sem, nz - 1)
     gap[0:outer, :] = start[:outer]
     gap[pl.ds(outer, outer), :] = start[outer:] + received(0)
     acc_ref[...] = jnp.zeros_like(acc_ref)
 
     def to_all(ref, send_sem, recv_sem):
-        def send(k, carry):
+        def send(to):
             pltpu.make_async_remote_copy(
                 src_ref=ref,
                 dst_ref=ref,
                 send_sem=send_sem,
                 recv_sem=recv_sem,
-                device_id=coords(k),
+                device_id=to,
                 device_id_type=MESH,
             ).start()
-            return carry
-
-        lax.fori_loop(1, devices, send, 0, unroll=devices <= 32)
+
+        if devices <= 32:
+            for a in range(nx):
+                for b in range(ny):
+                    for c in range(nz):
+                        if a or b or c:
+                            send((ids[0][a], ids[1][b], ids[2][c]))
+        else:
+
+            def step(k, carry):
+                send(coords(k))
+                return carry
+
+            lax.fori_loop(1, devices, step, 0)
 
     def lanes_sum(x):
         x = jnp.sum(x, axis=0, keepdims=True)
@@ -319,9 +380,8 @@
     def sweep(t, last):
         depth = jnp.where(live_rows, jnp.maximum(-gap[...], 0.0), 0.0)
         squares = lanes_sum(depth * depth)
-        if not last:
-            erecv[t, mine] = squares
-            to_all(erecv.at[t, mine], es_sem.at[t], er_sem.at[t])
+        erecv[t, mine] = squares
+        to_all(erecv.at[t, mine], es_sem.at[t], er_sem.at[t])
         for g in range(blocks // 8):
             lo, hi = 8 * g, 8 * g + 8
             terms = cat([depth[lo:hi] * geo[c, base + lo : base + hi] for c in range(3)])
@@ -338,18 +398,13 @@
         resid = jnp.sum(lanes_sum(near * near * first_col), axis=1, keepdims=True)
         rrecv[mine] = jnp.where(lane == t, resid, rrecv[mine])
         if last:
-            energy = jnp.sum(squares, axis=1, keepdims=True)
-            rrecv[mine] = jnp.where(lane == SWEEPS, energy, rrecv[mine])
             to_all(rrecv.at[mine], rs_sem, rr_sem)
-            others = rrecv.at[pl.ds(0, devices - 1)]
-            pltpu.make_async_copy(others, others, rr_sem).wait()
-            energy = jnp.sum(rrecv[...], axis=0)[:, SWEEPS : SWEEPS + 1]
         else:
             step = dots(base, 2 * blocks, moved)
             step = step[:blocks] + step[blocks:]
-            others = erecv.at[t, pl.ds(0, devices - 1)]
-            pltpu.make_async_copy(others, others, er_sem.at[t]).wait()
-            energy = jnp.sum(jnp.sum(erecv[t], axis=0), axis=1, keepdims=True)
+        others = erecv.at[t, pl.ds(0, devices - 1)]
+        pltpu.make_async_copy(others, others, er_sem.at[t]).wait()
+        energy = jnp.sum(jnp.sum(erecv[t], axis=0), axis=1, keepdims=True)
         scale = 1.0 / (1.0 + energy / (blocks * pairs * devices))
         hist_ref[0:1, :] = jnp.where(lane == t, energy, hist_ref[0:1, :])
         hist_ref[1:2, :] = jnp.where(lane == t, scale, hist_ref[1:2, :])
@@ -382,7 +437,9 @@
             for t in range(SWEEPS):
                 answer(t, d, axis, sign).wait_send()
 
-    for t in range(SWEEPS - 1):
+    others = rrecv.at[pl.ds(0, devices - 1)]
+    pltpu.make_async_copy(others, others, rr_sem).wait()
+    for t in range(SWEEPS):
         ref = erecv.at[t, pl.ds(0, devices - 1)]
         pltpu.make_async_copy(ref, ref, es_sem.at[t]).wait()
     others = rrecv.at[pl.ds(0, devices - 1)]
@@ -419,9 +476,15 @@
             jax.ShapeDtypeStruct((blocks, 3 * blk[2]), f32),
             jax.ShapeDtypeStruct((8, 128), f32),
         ),
-        in_specs=[vmem] * 6 + [pl.BlockSpec(memory_space=pl.ANY)],
+        in_specs=[pl.BlockSpec(memory_space=pl.ANY)] * 7,
         out_specs=(vmem, vmem),
         scratch_shapes=[
+            pltpu.VMEM(live_blocks.shape, jnp.int32),
+            pltpu.VMEM(pair_node.shape, jnp.int32),
+            pltpu.VMEM(pair_line.shape, jnp.int32),
+            pltpu.VMEM(pair_far.shape, jnp.int32),
+            pltpu.VMEM(far_line.shape, jnp.int32),
+            pltpu.VMEM(pair_geom.shape, f32),
             pltpu.VMEM(positions.shape, f32),
             pltpu.VMEM((4 * (pairs // 128) + 1, outer, 128), f32),
             pltpu.VMEM((2, blocks, pairs), f32),
@@ -439,7 +502,9 @@
             pltpu.VMEM((SWEEPS, 6, outer, pairs), f32),
             pltpu.VMEM((SWEEPS, devices, 1, 128), f32),
             pltpu.VMEM((devices, 1, 128), f32),
-            dma,
+            dma((7,)),
+            pltpu.SemaphoreType.REGULAR,
+            pltpu.SemaphoreType.REGULAR,
             dma((6,)),
             dma((6,)),
             dma((SWEEPS, 6)),
@@ -449,7 +514,7 @@
             dma,
             dma,
         ],
-        compiler_params=pltpu.CompilerParams(has_side_effects=True),
+        compiler_params=pltpu.CompilerParams(collective_id=0, has_side_effects=True),
     )(live_blocks, pair_node, pair_line, pair_far, far_line, pair_geom, positions)
     return pl.pallas_call(
         finish,

time: 52.2 us -> 45.4 us (0.87)
  Pallas kernels: 50.7 us -> 44 us
    pallas_call x1, Pallas kernels: 47.5 us -> 40.7 us  [local(): pl.pallas_call(functools.partial(kernel, sizes, blk), out_shape=(jax.Shap...]
where the time goes in v1:
time: 45.4 us; the launch traced here: 45.2 us
  Pallas kernels  44 us (97%)
  between operations  1.29 us (3%)
    pallas_call x1, Pallas kernels, local(): pl.pallas_call(functools.partial(kernel, sizes, blk), out_shape=(jax.Shap...  40.7 us
    pallas_call x1, Pallas kernels, local(): pl.pallas_call(finish, grid=(3,), out_shape=(jax.ShapeDtypeStruct(positio...  3.24 us

profile of v1, /device:TPU:0, one launch (start us, length us, event | category | flops | bytes accessed | tf_op | source)
XLA Modules:
  0.0 45.2 jit_solution(6790780184537414931)
XLA Ops:
  1.3 40.7 %shard_map.86 = (f32[32,768]{1,0:T(8,128)}, f32[8,128]{1,0:T(8,128)}) custom-call(s32[1,1,1]{2,1,0:T(1,128)S(6)} %copy.9.live_hbm, s32[1,1,1,32,256]{4,3,2,1,0:T(8,128)} %node_hbm.1, s32[1,1,1,32]{3,2,1,0:T(1,128)} %line_ref.1, s32[1,1,1,32,256]{4,3,2,1,0:T(8,128)} %farpos_hbm.1, s32[1,1,1,32]{3,2,1,0:T(1,128)} %farline_hbm.1, ...), custom_call_target="tpu_custom_call" | custom-call | tf_op jit(solution)/shard_map/pallas_call | solution.py:473
  42.0 3.2 %shard_map.87 = (f32[3,16,16,256]{3,2,1,0:T(8,128)}, f32[2,5]{1,0:T(2,128)}) custom-call(f32[32,768]{1,0:T(8,128)} %get-tuple-element.4.acc_ref, s32[1,1,1,32]{3,2,1,0:T(1,128)} %line_ref.1, f32[8,128]{1,0:T(8,128)} %get-tuple-element.5.hist_in, f32[3,16,16,256]{3,2,1,0:T(8,128)} %pos_ref.1), custom_call_target="tpu_custom_call" | custom-call | tf_op jit(solution)/shard_map/pallas_call | solution.py:519

commit v2 on v1

--- a/solution.py
+++ b/solution.py
@@ -1,4 +1,5 @@
 import functools
+import itertools
 
 import jax
 import jax.numpy as jnp
@@ -30,39 +31,51 @@
     return jnp.dot(a, b, preferred_element_type=f32)
 
 
-def take_lanes(x, low, half):
-    outs = []
+def near_radii(sizes):
+    need = max(sizes[0] - 1, sizes[1] + sizes[2] - 2)
+    radii = [1]
+    while 2 * radii[-1] < need:
+        radii.append(2 * radii[-1])
+    return radii
+
+
+def take_lanes(xs, low, half):
+    outs = [[] for _ in xs]
     for h in range(0, low.shape[1], 128):
         idx = low[:, h : h + 128]
-        got = jnp.take_along_axis(x[:, :128], idx, axis=1, mode="promise_in_bounds")
-        for j in range(1, x.shape[1] // 128):
-            more = jnp.take_along_axis(
-                x[:, 128 * j : 128 * (j + 1)], idx, axis=1, mode="promise_in_bounds"
-            )
-            got = jnp.where(half[:, h : h + 128] == j, more, got)
-        outs.append(got)
-    return jnp.concatenate(outs, axis=1)
+        got = [None] * len(xs)
+        for j in range(xs[0].shape[1] // 128):
+            for i, x in enumerate(xs):
+                more = jnp.take_along_axis(
+                    x[:, 128 * j : 128 * (j + 1)], idx, axis=1, mode="promise_in_bounds"
+                )
+                got[i] = jnp.where(half[:, h : h + 128] == j, more, got[i]) if j else more
+        for out, x in zip(outs, got):
+            out.append(x)
+    return [jnp.concatenate(out, axis=1) for out in outs]
 
 
 def kernel(
     sizes,
     blk,
-    live_hbm,
+    live_ref,
     node_hbm,
     line_hbm,
     farpos_hbm,
     farline_hbm,
     geom_hbm,
     pos_hbm,
-    acc_ref,
-    hist_ref,
-    live_ref,
+    out_ref,
+    hist_out,
     node_ref,
     line_ref,
     farpos_ref,
     farline_ref,
     geom_ref,
     pos_ref,
+    acc_ref,
+    hist_ref,
+    step_ref,
     req,
     cols,
     hot,
@@ -80,7 +93,7 @@
     erecv,
     rrecv,
     in_sem,
-    plane_sem,
+    near_sem,
     whole_sem,
     qs_sem,
     qr_sem,
@@ -119,15 +132,33 @@
 
     ids = [[moved_by(a, k) for k in range(sizes[a])] for a in range(3)]
 
-    def signal_line(sem, axis):
-        for k in range(1, sizes[axis]):
-            to = list(me)
-            to[axis] = ids[axis][k]
-            pl.semaphore_signal(sem, inc=1, device_id=tuple(to), device_id_type=MESH)
-
+    def sphere(r):
+        steps = itertools.product(*[range(1 - n, n) for n in sizes])
+        return [s for s in steps if sum(abs(x) for x in s) == r]
+
+    def inside(step):
+        ok = True
+        for x, n, at in zip(step, sizes, me):
+            if x > 0:
+                ok = ok & (at < n - x)
+            if x < 0:
+                ok = ok & (at >= -x)
+        return ok
+
+    def signal_sphere(sem, r):
+        for step in sphere(r):
+
+            @pl.when(inside(step))
+            def _():
+                to = tuple(at + x for at, x in zip(me, step))
+                pl.semaphore_signal(sem, inc=1, device_id=to, device_id_type=MESH)
+
+    def wait_sphere(sem, r):
+        pl.semaphore_wait(sem, sum(jnp.where(inside(s), 1, 0) for s in sphere(r)))
+
+    radii = near_radii(sizes)
     barrier = pltpu.get_barrier_semaphore()
-    for axis in range(3):
-        signal_line(barrier, axis)
+    signal_sphere(barrier, 1)
     inputs = [
         pltpu.make_async_copy(src, dst, in_sem.at[i])
         for i, (src, dst) in enumerate(
@@ -137,7 +168,6 @@
                 (geom_hbm, geom_ref),
                 (node_hbm, node_ref),
                 (line_hbm, line_ref),
-                (live_hbm, live_ref),
                 (pos_hbm, pos_ref),
             ]
         )
@@ -170,15 +200,15 @@
             device_id_type=MESH,
         )
 
-    pl.semaphore_wait(barrier, sum(sizes) - 3)
+    wait_sphere(barrier, 1)
     for d, (axis, sign) in enumerate(dirs):
 
         @pl.when(exists(axis, sign))
         def _():
             ask(d, axis, sign).start()
 
-    signal_line(plane_sem, 0)
-    for copy in inputs[3:6]:
+    signal_sphere(near_sem.at[0], radii[0])
+    for copy in inputs[3:5]:
         copy.wait()
     cols[0] = column(line_ref)
 
@@ -193,11 +223,14 @@
             for t in range(SWEEPS):
                 drecv[t, d] = jnp.zeros((outer, pairs), f32)
 
-    live = jnp.broadcast_to(live_ref[0], (blocks, pairs))
-    live_rows = lax.broadcasted_iota(jnp.int32, (blocks, pairs), 0) < live
+    live_rows = lax.broadcasted_iota(jnp.int32, (blocks, pairs), 0) < live_ref[0, 0, 0]
     lane_node = lax.broadcasted_iota(jnp.int32, (pairs, bz), 1).astype(f32)
     node_t = jnp.transpose(node_ref[0, 0, 0].astype(f32))
     for b in range(blocks):
+        if b == outer:
+            wait_sphere(near_sem.at[0], radii[0])
+            if len(radii) > 1:
+                signal_sphere(near_sem.at[1], radii[1])
         hot[pl.ds(b * pairs, pairs), :] = jnp.where(
             node_t[:, b : b + 1] == lane_node, 1.0, 0.0
         ).astype(bf16)
@@ -245,28 +278,22 @@
         low_ref[pl.ds(row, n), :] = low
         half_ref[pl.ds(row, n), :] = half
         own = jnp.where(line == lane_line, 1.0, 0.0).astype(bf16)
-        total = jnp.zeros((n, pairs), f32)
+        vals = []
         for c in range(3):
             geo[c, pl.ds(row, n), :] = geom[c]
-            vals = jnp.zeros((n, bz), f32)
-            for part in split(pos_ref[c].reshape(lines, bz), 3):
-                vals += mm(own, part)
-            total += geom[c] * take_lanes(vals, low, half)
-        return total
+            vals.append(sum(mm(own, part) for part in split(pos_ref[c].reshape(lines, bz), 3)))
+        return sum(g * x for g, x in zip(geom, take_lanes(vals, low, half)))
 
     def cat(parts):
         return jnp.concatenate(parts, axis=0)
 
-    inputs[6].wait()
+    inputs[5].wait()
     for d, (axis, sign) in enumerate(dirs):
 
         @pl.when(exists(axis, -sign))
         def _():
             ask(d, axis, sign).wait_recv()
 
-    if nx > 1:
-        pl.semaphore_wait(plane_sem, nx - 1)
-    signal_line(whole_sem, 2)
     asked = []
     for d, (axis, sign) in enumerate(dirs):
         shift = [0, 0, 0]
@@ -285,8 +312,7 @@
 
     def respond(t, total):
         for d, (axis, sign) in enumerate(dirs):
-            dsend[t, d] = total[d * outer : (d + 1) * outer]
-        for d, (axis, sign) in enumerate(dirs):
+            dsend[t, d] = total(d * outer, outer)
 
             @pl.when(exists(axis, -sign))
             def _():
@@ -314,7 +340,15 @@
             got = got + drecv[t, d]
         return got
 
-    respond(0, setup(0, asked[0], asked[1], asked[2:]))
+    first = setup(0, asked[0], asked[1], asked[2:])
+    respond(0, lambda row, n: first[row : row + n])
+    for i, r in enumerate(radii[1:], 1):
+        wait_sphere(near_sem.at[i], r)
+        if i + 1 < len(radii):
+            signal_sphere(near_sem.at[i + 1], radii[i + 1])
+    for k in range(1, nx):
+        to = (ids[0][k], me[1], me[2])
+        pl.semaphore_signal(whole_sem, inc=1, device_id=to, device_id_type=MESH)
 
     line, z, ok = located(cols[1], farpos_ref[0, 0, 0].astype(f32), (0, 0, 0))
     geom = [geom_ref[0, 0, 0, :, c, :] for c in range(4)]
@@ -325,8 +359,8 @@
         [cat([geom[c], jnp.where(ok, -geom[c], 0.0)]) for c in range(3)],
     )
     start = start[:blocks] + start[blocks:] - geom[3]
-    if nz > 1:
-        pl.semaphore_wait(whole_sem, nz - 1)
+    if nx > 1:
+        pl.semaphore_wait(whole_sem, nx - 1)
     gap[0:outer, :] = start[:outer]
     gap[pl.ds(outer, outer), :] = start[outer:] + received(0)
     acc_ref[...] = jnp.zeros_like(acc_ref)
@@ -364,6 +398,11 @@
         return out
 
     lane = lax.broadcasted_iota(jnp.int32, (1, 128), 1)
+    at_line = lax.broadcasted_iota(jnp.int32, (lines, 2 * blocks), 0).astype(f32)
+    place = jnp.where(at_line == two[...], 1.0, 0.0).astype(bf16)
+
+    def placed(x):
+        return mm(place, cat(split(x, 2)))
 
     def apply(row, n, parts):
         both = mm(amat[row : row + n, :], parts)
@@ -372,10 +411,8 @@
     def dots(row, n, moved):
         low = low_ref[row : row + n, :]
         half = half_ref[row : row + n, :]
-        total = geo[0, row : row + n] * take_lanes(moved[0], low, half)
-        for c in range(1, 3):
-            total += geo[c, row : row + n] * take_lanes(moved[c], low, half)
-        return total
+        got = take_lanes(moved, low, half)
+        return sum(geo[c, row : row + n] * got[c] for c in range(3))
 
     def sweep(t, last):
         depth = jnp.where(live_rows, jnp.maximum(-gap[...], 0.0), 0.0)
@@ -392,13 +429,21 @@
                 wcat[lo:hi, c * bz : (c + 1) * bz] = sums[8 * c : 8 * c + 8]
         parts = cat(split(wcat[...], 2))
         if not last:
-            respond(t + 1, dots(0, base, apply(0, base, parts)))
+            far = apply(0, base, parts)
+            respond(
+                t + 1, lambda row, n: dots(row, n, [m[row : row + n] for m in far])
+            )
         moved = apply(base, blocks if last else 2 * blocks, parts)
         near = jnp.concatenate([m[:blocks] for m in moved], axis=1)
         resid = jnp.sum(lanes_sum(near * near * first_col), axis=1, keepdims=True)
         rrecv[mine] = jnp.where(lane == t, resid, rrecv[mine])
         if last:
             to_all(rrecv.at[mine], rs_sem, rr_sem)
+            for c in range(3):
+                cut = slice(c * bz, (c + 1) * bz)
+                done = placed(acc_ref[:, cut])
+                out_ref[c] = pos_ref[c] + done.reshape(bx, by, bz)
+                step_ref[c] = placed(first_col * near[:, cut]).reshape(bx, by, bz)
         else:
             step = dots(base, 2 * blocks, moved)
             step = step[:blocks] + step[blocks:]
@@ -408,8 +453,11 @@
         scale = 1.0 / (1.0 + energy / (blocks * pairs * devices))
         hist_ref[0:1, :] = jnp.where(lane == t, energy, hist_ref[0:1, :])
         hist_ref[1:2, :] = jnp.where(lane == t, scale, hist_ref[1:2, :])
-        acc_ref[...] = acc_ref[...] + (scale * first_col) * near
-        if not last:
+        if last:
+            for c in range(3):
+                out_ref[c] = out_ref[c] + scale[:, :, None] * step_ref[c]
+        else:
+            acc_ref[...] = acc_ref[...] + (scale * first_col) * near
             more = received(t + 1)
             gap[0:outer, :] = gap[0:outer, :] + scale * step[:outer]
             gap[pl.ds(outer, outer), :] = gap[pl.ds(outer, outer), :] + scale * (
@@ -446,20 +494,20 @@
     pltpu.make_async_copy(others, others, rs_sem).wait()
     energy, scale = hist_ref[0:1, :], hist_ref[1:2, :]
     resid = jnp.sum(rrecv[...], axis=0)
-    hist_ref[0:1, :] = jnp.sqrt(1.0 + energy / (blocks * pairs))
-    hist_ref[1:2, :] = jnp.sqrt(1.0 + scale * scale * resid / (bx * by * bz))
-
-
-def finish(acc_ref, line_ref, hist_in, pos_ref, out_ref, hist_ref):
-    _, bx, by, bz = pos_ref.shape
-    lines = bx * by
-    row = line_ref[0, 0].astype(f32)
-    row = jnp.concatenate([row, row], axis=1)
-    rows = lax.broadcasted_iota(jnp.int32, (lines, row.shape[1]), 0).astype(f32)
-    place = jnp.where(rows == row, 1.0, 0.0).astype(bf16)
-    total = mm(place, jnp.concatenate(split(acc_ref[...], 2), axis=0))
-    out_ref[0] = pos_ref[0] + total.reshape(bx, by, bz)
-    hist_ref[...] = hist_in[0:2, : hist_ref.shape[1]]
+    hist_out[0:1, :] = jnp.sqrt(1.0 + energy / (blocks * pairs))[:, :SWEEPS]
+    resid = scale * scale * resid / (bx * by * bz)
+    hist_out[1:2, :] = jnp.sqrt(1.0 + resid)[:, :SWEEPS]
+
+
+def finish(pos_ref, hist_ref, pos_out, hist_out, sem):
+    copies = [
+        pltpu.make_async_copy(pos_ref, pos_out, sem.at[0]),
+        pltpu.make_async_copy(hist_ref, hist_out, sem.at[1]),
+    ]
+    for copy in copies:
+        copy.start()
+    for copy in copies:
+        copy.wait()
 
 
 def local(sizes, positions, pair_node, pair_line, pair_far, far_line, pair_geom, live_blocks):
@@ -473,18 +521,21 @@
     moved, hist = pl.pallas_call(
         functools.partial(kernel, sizes, blk),
         out_shape=(
-            jax.ShapeDtypeStruct((blocks, 3 * blk[2]), f32),
-            jax.ShapeDtypeStruct((8, 128), f32),
+            pltpu.VMEM(positions.shape, f32),
+            pltpu.VMEM((2, SWEEPS), f32),
         ),
-        in_specs=[pl.BlockSpec(memory_space=pl.ANY)] * 7,
+        in_specs=[pl.BlockSpec(memory_space=pltpu.SMEM)]
+        + [pl.BlockSpec(memory_space=pltpu.HBM)] * 6,
         out_specs=(vmem, vmem),
         scratch_shapes=[
-            pltpu.VMEM(live_blocks.shape, jnp.int32),
             pltpu.VMEM(pair_node.shape, jnp.int32),
             pltpu.VMEM(pair_line.shape, jnp.int32),
             pltpu.VMEM(pair_far.shape, jnp.int32),
             pltpu.VMEM(far_line.shape, jnp.int32),
             pltpu.VMEM(pair_geom.shape, f32),
+            pltpu.VMEM(positions.shape, f32),
+            pltpu.VMEM((blocks, 3 * blk[2]), f32),
+            pltpu.VMEM((8, 128), f32),
             pltpu.VMEM(positions.shape, f32),
             pltpu.VMEM((4 * (pairs // 128) + 1, outer, 128), f32),
             pltpu.VMEM((2, blocks, pairs), f32),
@@ -502,8 +553,8 @@
             pltpu.VMEM((SWEEPS, 6, outer, pairs), f32),
             pltpu.VMEM((SWEEPS, devices, 1, 128), f32),
             pltpu.VMEM((devices, 1, 128), f32),
-            dma((7,)),
-            pltpu.SemaphoreType.REGULAR,
+            dma((6,)),
+            pltpu.SemaphoreType.REGULAR((len(near_radii(sizes)),)),
             pltpu.SemaphoreType.REGULAR,
             dma((6,)),
             dma((6,)),
@@ -514,26 +565,34 @@
             dma,
             dma,
         ],
-        compiler_params=pltpu.CompilerParams(collective_id=0, has_side_effects=True),
-    )(live_blocks, pair_node, pair_line, pair_far, far_line, pair_geom, positions)
+        compiler_params=pltpu.CompilerParams(
+            collective_id=0, has_side_effects=True, vmem_limit_bytes=40 << 20
+        ),
+    )(
+        live_blocks,
+        *[
+            pltpu.with_memory_space_constraint(x, pltpu.HBM)
+            for x in (
+                pair_node,
+                pair_line,
+                pair_far,
+                far_line,
+                pair_geom,
+                positions,
+            )
+        ]
+    )
     return pl.pallas_call(
         finish,
-        grid=(3,),
         out_shape=(
             jax.ShapeDtypeStruct(positions.shape, f32),
             jax.ShapeDtypeStruct((2, SWEEPS), f32),
         ),
-        in_specs=[
-            pl.BlockSpec((blocks, blk[2]), lambda c: (0, c)),
-            pl.BlockSpec(pair_line.shape, lambda c: (0, 0, 0, 0)),
-            pl.BlockSpec((8, 128), lambda c: (0, 0)),
-            pl.BlockSpec((1,) + blk, lambda c: (c, 0, 0, 0)),
-        ],
-        out_specs=(
-            pl.BlockSpec((1,) + blk, lambda c: (c, 0, 0, 0)),
-            pl.BlockSpec((2, SWEEPS), lambda c: (0, 0)),
-        ),
-    )(moved, pair_line, hist, positions)
+        in_specs=[vmem] * 2,
+        out_specs=[pl.BlockSpec(memory_space=pl.ANY)] * 2,
+        scratch_shapes=[dma((2,))],
+        compiler_params=pltpu.CompilerParams(vmem_limit_bytes=1 << 20),
+    )(moved, hist)
 
 
 def solution(mesh):

time: 45.4 us -> 41.2 us (0.907)
  Pallas kernels: 44 us -> 39.7 us
    pallas_call x2, Pallas kernels: 44 us -> 39.7 us  [the longest x1 38.8 us: local(): pl.pallas_call(functools.partial(kernel, sizes, blk), out_shape=(pltpu.VM...]
where the time goes in v2:
time: 41.2 us; the launch traced here: 41 us
  Pallas kernels  39.7 us (96%)
  between operations  1.29 us (3%)
    pallas_call x1, Pallas kernels, local(): pl.pallas_call(functools.partial(kernel, sizes, blk), out_shape=(pltpu.VM...  38.8 us
    pallas_call x1, Pallas kernels, local(): pl.pallas_call(finish, out_shape=(jax.ShapeDtypeStruct(positions.shape, f...  0.9 us

profile of v2, /device:TPU:0, one launch (start us, length us, event | category | flops | bytes accessed | tf_op | source)
XLA Modules:
  0.0 41.0 jit_solution(16937324614678813948)
XLA Ops:
  1.3 38.8 %shard_map.86 = (f32[3,16,16,256]{3,2,1,0:T(8,128)S(1)}, f32[2,5]{1,0:T(2,128)S(1)}) custom-call(s32[1,1,1]{2,1,0:T(1,128)S(6)} %copy.9.live_ref, s32[1,1,1,32,256]{4,3,2,1,0:T(8,128)} %node_hbm.1, s32[1,1,1,32]{3,2,1,0:T(1,128)} %line_hbm.1, s32[1,1,1,32,256]{4,3,2,1,0:T(8,128)} %farpos_hbm.1, s32[1,1,1,32]{3,2,1,0:T(1,128)} %farline_hbm.1, ...), custom_call_target="tpu_custom_call" | custom-call | tf_op jit(solution)/shard_map/pallas_call | solution.py:521
  40.1 0.9 %shard_map.87 = (f32[3,16,16,256]{3,2,1,0:T(8,128)}, f32[2,5]{1,0:T(2,128)}) custom-call(f32[3,16,16,256]{3,2,1,0:T(8,128)S(1)} %get-tuple-element.4.pos_ref, f32[2,5]{1,0:T(2,128)S(1)} %get-tuple-element.5.hist_ref), custom_call_target="tpu_custom_call" | custom-call | tf_op jit(solution)/shard_map/pallas_call | solution.py:585

commit v3 on v2

--- a/solution.py
+++ b/solution.py
@@ -74,8 +74,13 @@
     geom_ref,
     pos_ref,
     acc_ref,
-    hist_ref,
+    near_ref,
     step_ref,
+    pos3,
+    code,
+    codes,
+    lsend,
+    lrecv,
     req,
     cols,
     hot,
@@ -86,7 +91,8 @@
     low_ref,
     half_ref,
     gap,
-    wcat,
+    terms,
+    sums,
     reqs,
     dsend,
     drecv,
@@ -95,14 +101,10 @@
     in_sem,
     near_sem,
     whole_sem,
-    qs_sem,
-    qr_sem,
     ds_sem,
     dr_sem,
     es_sem,
     er_sem,
-    rs_sem,
-    rr_sem,
 ):
     nx, ny, nz = sizes
     bx, by, bz = blk
@@ -188,24 +190,37 @@
         for h in range(wide):
             req[c * wide + h] = planes[c][:, 128 * h : 128 * (h + 1)]
     cols[1] = column(farline_ref)
-    req[4 * wide] = cols[1, outer:, :128]
-
-    def ask(d, axis, sign):
+    code[...] = cols[1, outer:, :128]
+
+    def remote(src, dst, slot, d, to):
         return pltpu.make_async_remote_copy(
-            src_ref=req,
-            dst_ref=reqs.at[d],
-            send_sem=qs_sem.at[d],
-            recv_sem=qr_sem.at[d],
-            device_id=neighbour(axis, sign),
+            src_ref=src,
+            dst_ref=dst,
+            send_sem=ds_sem.at[slot, d],
+            recv_sem=dr_sem.at[slot, d],
+            device_id=neighbour(*to),
             device_id_type=MESH,
         )
 
+    def ask_line(d, axis, sign):
+        return remote(code, codes.at[d], 2, d, (axis, sign))
+
+    def ask_pairs(d, axis, sign):
+        return remote(req, reqs.at[d], 3, d, (axis, sign))
+
+    def line_back(d, axis, sign):
+        return remote(lsend.at[d], lrecv.at[d], 0, d, (axis, -sign))
+
+    def answer(t, d, axis, sign):
+        return remote(dsend.at[t, d], drecv.at[t, d], t % 2, d, (axis, -sign))
+
     wait_sphere(barrier, 1)
-    for d, (axis, sign) in enumerate(dirs):
-
-        @pl.when(exists(axis, sign))
-        def _():
-            ask(d, axis, sign).start()
+    for ask in (ask_line, ask_pairs):
+        for d, (axis, sign) in enumerate(dirs):
+
+            @pl.when(exists(axis, sign))
+            def _():
+                ask(d, axis, sign).start()
 
     signal_sphere(near_sem.at[0], radii[0])
     for copy in inputs[3:5]:
@@ -216,16 +231,25 @@
 
         @pl.when(jnp.logical_not(exists(axis, -sign)))
         def _():
+            codes[d] = jnp.zeros(code.shape, f32)
             reqs[d] = jnp.zeros(req.shape, f32)
 
         @pl.when(jnp.logical_not(exists(axis, sign)))
         def _():
-            for t in range(SWEEPS):
+            lrecv[d] = jnp.zeros((3, outer, bz), f32)
+            for t in range(1, SWEEPS):
                 drecv[t, d] = jnp.zeros((outer, pairs), f32)
 
+    def at_lanes(z):
+        z = z.astype(jnp.int32)
+        return lax.bitwise_and(z, 127), lax.shift_right_arithmetic(z, 7)
+
     live_rows = lax.broadcasted_iota(jnp.int32, (blocks, pairs), 0) < live_ref[0, 0, 0]
-    lane_node = lax.broadcasted_iota(jnp.int32, (pairs, bz), 1).astype(f32)
-    node_t = jnp.transpose(node_ref[0, 0, 0].astype(f32))
+    node_low, node_half = at_lanes(node_ref[0, 0, 0])
+    lane_node = lax.broadcasted_iota(jnp.int32, (pairs, 128), 1).astype(f32)
+    node_t = jnp.transpose(node_low.astype(f32))
+    group = terms.shape[1] // blocks
+    terms[...] = jnp.zeros_like(terms)
     for b in range(blocks):
         if b == outer:
             wait_sphere(near_sem.at[0], radii[0])
@@ -244,18 +268,29 @@
         jnp.where(same & (col_mod < row_mod), 1.0, 0.0), axis=1, keepdims=True
     )
 
-    def expand(stack, step):
-        rows = stack.shape[0]
-        which = lax.rem(lax.broadcasted_iota(jnp.int32, (rows, pairs), 0), step)
-        return jnp.concatenate(
-            [jnp.where(which == j, stack, 0.0).astype(bf16) for j in range(step)], axis=1
-        )
-
-    counts = []
-    for g in range(blocks // 8):
-        ones = jnp.where(live_rows[8 * g : 8 * g + 8], 1.0, 0.0)
-        counts.append(mm(expand(ones, 8), hot[pl.ds(8 * g * pairs, 8 * pairs), :]))
-    counts = jnp.concatenate(counts, axis=0).astype(bf16)
+    def cat(parts, axis=0):
+        return jnp.concatenate(parts, axis=axis)
+
+    def scatter(values):
+        n = len(values)
+        for h in range(bz // 128):
+            for c in range(n):
+                x = jnp.where(node_half == h, values[c], 0.0)
+                for j in range(wide):
+                    cut = x[:, 128 * j : 128 * (j + 1)]
+                    terms[j, pl.ds(h * n + c, blocks, stride=group), :] = cut
+        for b in range(blocks):
+            slot = cat([terms[j, pl.ds(b * group, group), :] for j in range(wide)], 1)
+            both = cat(split(slot, 2))
+            both = mm(both, hot[pl.ds(b * pairs, pairs), :])
+            sums[pl.ds(b * group, group), :] = both[:group] + both[group:]
+        return [
+            cat([sums[pl.ds(h * n + c, blocks, stride=group), :] for h in range(bz // 128)], 1)
+            for c in range(n)
+        ]
+
+    ones = jnp.where(live_rows, 1.0, 0.0)
+    counts = scatter([ones, jnp.zeros_like(ones), jnp.zeros_like(ones)])[0].astype(bf16)
 
     def located(code, zpos, shift):
         e = jnp.floor((code + 0.5) / (by + 2 * RIM))
@@ -268,80 +303,60 @@
 
     def setup(row, line, node, geom):
         n = line.shape[0]
-        lane_line = lax.broadcasted_iota(jnp.int32, (n, lines), 1).astype(f32)
         a = jnp.where(line[:, : 2 * blocks] == two[...], 1.0, 0.0).astype(bf16)
         amat[pl.ds(row, n), :] = a
         cinv[pl.ds(row, n), :] = RELAX / (1.0 + mm(a[:, :blocks], counts))
-        idx = node.astype(jnp.int32)
-        low = lax.bitwise_and(idx, 127)
-        half = lax.shift_right_logical(idx, 7)
+        low, half = at_lanes(node)
         low_ref[pl.ds(row, n), :] = low
         half_ref[pl.ds(row, n), :] = half
-        own = jnp.where(line == lane_line, 1.0, 0.0).astype(bf16)
-        vals = []
         for c in range(3):
             geo[c, pl.ds(row, n), :] = geom[c]
-            vals.append(sum(mm(own, part) for part in split(pos_ref[c].reshape(lines, bz), 3)))
-        return sum(g * x for g, x in zip(geom, take_lanes(vals, low, half)))
-
-    def cat(parts):
-        return jnp.concatenate(parts, axis=0)
-
+
+    def fetch(line):
+        lane_line = lax.broadcasted_iota(jnp.int32, (line.shape[0], lines), 1).astype(f32)
+        own = jnp.where(line == lane_line, 1.0, 0.0).astype(bf16)
+        return [sum(mm(own, pos3[c, k]) for k in range(3)) for c in range(3)]
+
+    base = len(dirs) * outer
+    rows = base + 2 * blocks
+    node = node_ref[0, 0, 0].astype(f32)
+    far = farpos_ref[0, 0, 0].astype(f32)
+    geom = [geom_ref[0, 0, 0, :, c, :] for c in range(4)]
+    line, z, ok = located(cols[1], far, (0, 0, 0))
+    setup(
+        base,
+        cat([line_b, line]),
+        cat([node, jnp.where(ok, z, 0.0)]),
+        [cat([geom[c], jnp.where(ok, -geom[c], 0.0)]) for c in range(3)],
+    )
     inputs[5].wait()
+    for c in range(3):
+        for k, part in enumerate(split(pos_ref[c].reshape(lines, bz), 3)):
+            pos3[c, k] = part
+    vals = fetch(cat([line_b, line]))
+
     for d, (axis, sign) in enumerate(dirs):
 
         @pl.when(exists(axis, -sign))
         def _():
-            ask(d, axis, sign).wait_recv()
-
+            ask_line(d, axis, sign).wait_recv()
+
+    shifts = []
+    for axis, sign in dirs:
+        shifts.append([sign if a == axis else 0 for a in range(3)])
     asked = []
+    for d in range(len(dirs)):
+        there = jnp.concatenate([codes[d]] * wide, axis=1)
+        asked.append(located(there, 0.0, shifts[d])[0])
+    back = fetch(cat(asked))
     for d, (axis, sign) in enumerate(dirs):
-        shift = [0, 0, 0]
-        shift[axis] = sign
-        got = [
-            jnp.concatenate([reqs[d, c * wide + h] for h in range(wide)], axis=1) for c in range(4)
-        ]
-        code = jnp.concatenate([reqs[d, 4 * wide]] * wide, axis=1)
-        line, z, ok = located(code, got[3], shift)
-        asked.append(
-            [line, jnp.where(ok, z, 0.0)] + [jnp.where(ok, -got[c], 0.0) for c in range(3)]
-        )
-    asked = [cat([x[i] for x in asked]) for i in range(5)]
-    base = asked[0].shape[0]
-    rows = base + 2 * blocks
-
-    def respond(t, total):
-        for d, (axis, sign) in enumerate(dirs):
-            dsend[t, d] = total(d * outer, outer)
-
-            @pl.when(exists(axis, -sign))
-            def _():
-                answer(t, d, axis, sign).start()
-
-    def answer(t, d, axis, sign):
-        return pltpu.make_async_remote_copy(
-            src_ref=dsend.at[t, d],
-            dst_ref=drecv.at[t, d],
-            send_sem=ds_sem.at[t, d],
-            recv_sem=dr_sem.at[t, d],
-            device_id=neighbour(axis, -sign),
-            device_id_type=MESH,
-        )
-
-    def received(t):
-        for d, (axis, sign) in enumerate(dirs):
-
-            @pl.when(exists(axis, sign))
-            def _():
-                answer(t, d, axis, sign).wait_recv()
-
-        got = drecv[t, 0]
-        for d in range(1, len(dirs)):
-            got = got + drecv[t, d]
-        return got
-
-    first = setup(0, asked[0], asked[1], asked[2:])
-    respond(0, lambda row, n: first[row : row + n])
+        for c in range(3):
+            lsend[d, c] = back[c][d * outer : (d + 1) * outer]
+
+        @pl.when(exists(axis, -sign))
+        def _():
+            line_back(d, axis, sign).start()
+
     for i, r in enumerate(radii[1:], 1):
         wait_sphere(near_sem.at[i], r)
         if i + 1 < len(radii):
@@ -350,19 +365,88 @@
         to = (ids[0][k], me[1], me[2])
         pl.semaphore_signal(whole_sem, inc=1, device_id=to, device_id_type=MESH)
 
-    line, z, ok = located(cols[1], farpos_ref[0, 0, 0].astype(f32), (0, 0, 0))
-    geom = [geom_ref[0, 0, 0, :, c, :] for c in range(4)]
-    start = setup(
-        base,
-        cat([line_b, line]),
-        cat([node_ref[0, 0, 0].astype(f32), jnp.where(ok, z, 0.0)]),
-        [cat([geom[c], jnp.where(ok, -geom[c], 0.0)]) for c in range(3)],
-    )
-    start = start[:blocks] + start[blocks:] - geom[3]
+    start = take_lanes([v[:blocks] for v in vals], *at_lanes(node))
+    inner = take_lanes([v[blocks : blocks + outer] for v in vals], *at_lanes(z[:outer]))
+    gap[...] = sum(geom[c] * start[c] for c in range(3)) - geom[3]
+    gap[0:outer, :] = gap[0:outer, :] - sum(geom[c][:outer] * inner[c] for c in range(3))
+
+    for d, (axis, sign) in enumerate(dirs):
+
+        @pl.when(exists(axis, -sign))
+        def _():
+            ask_pairs(d, axis, sign).wait_recv()
+
+    pairs_in = []
+    for d in range(len(dirs)):
+        got = [
+            jnp.concatenate([reqs[d, c * wide + h] for h in range(wide)], axis=1) for c in range(4)
+        ]
+        there = jnp.concatenate([codes[d]] * wide, axis=1)
+        _, at, ok = located(there, got[3], shifts[d])
+        pairs_in.append([jnp.where(ok, at, 0.0)] + [jnp.where(ok, -got[c], 0.0) for c in range(3)])
+    pairs_in = [cat([x[i] for x in pairs_in]) for i in range(4)]
+    setup(0, cat(asked), pairs_in[0], pairs_in[1:])
+
+    for d, (axis, sign) in enumerate(dirs):
+
+        @pl.when(exists(axis, sign))
+        def _():
+            line_back(d, axis, sign).wait_recv()
+
+    low, half = at_lanes(far[outer:] - RIM)
+    reach = []
+    for c in range(3):
+        line = vals[c][blocks + outer :]
+        for d, (axis, sign) in enumerate(dirs):
+            if axis < 2:
+                line = line + lrecv[d, c]
+        below = lrecv[dirs.index((2, -1)), c][:, bz - 128 :]
+        above = lrecv[dirs.index((2, 1)), c][:, :128]
+        reach.append(jnp.concatenate([below, line, above], axis=1))
+    reach = take_lanes(reach, low, half + 1)
     if nx > 1:
         pl.semaphore_wait(whole_sem, nx - 1)
-    gap[0:outer, :] = start[:outer]
-    gap[pl.ds(outer, outer), :] = start[outer:] + received(0)
+    gap[pl.ds(outer, outer), :] = gap[pl.ds(outer, outer), :] - sum(
+        geom[c][outer:] * reach[c] for c in range(3)
+    )
+    for d, (axis, sign) in enumerate(dirs):
+
+        @pl.when(exists(axis, sign))
+        def _():
+            ask_line(d, axis, sign).wait_send()
+            ask_pairs(d, axis, sign).wait_send()
+
+        @pl.when(exists(axis, -sign))
+        def _():
+            line_back(d, axis, sign).wait_send()
+
+    def respond(t, total):
+        for d, (axis, sign) in enumerate(dirs):
+            dsend[t, d] = total(d * outer, outer)
+
+            @pl.when(exists(axis, -sign))
+            def _():
+                answer(t, d, axis, sign).start()
+
+    def responded(t):
+        for d, (axis, sign) in enumerate(dirs):
+
+            @pl.when(exists(axis, -sign))
+            def _():
+                answer(t, d, axis, sign).wait_send()
+
+    def received(t):
+        for d, (axis, sign) in enumerate(dirs):
+
+            @pl.when(exists(axis, sign))
+            def _():
+                answer(t, d, axis, sign).wait_recv()
+
+        got = drecv[t, 0]
+        for d in range(1, len(dirs)):
+            got = got + drecv[t, d]
+        return got
+
     acc_ref[...] = jnp.zeros_like(acc_ref)
 
     def to_all(ref, send_sem, recv_sem):
@@ -414,31 +498,36 @@
         got = take_lanes(moved, low, half)
         return sum(geo[c, row : row + n] * got[c] for c in range(3))
 
-    def sweep(t, last):
+    def wait_all(ref, sem):
+        others = ref.at[pl.ds(0, devices - 1)]
+        pltpu.make_async_copy(others, others, sem).wait()
+
+    def settle(scale):
+        acc_ref[...] = acc_ref[...] + (scale * first_col) * near_ref[...]
+
+    rrecv[mine] = jnp.zeros((1, 128), f32)
+    energies, scales = [], []
+    for t in range(SWEEPS):
+        last, slot = t == SWEEPS - 1, t % 2
         depth = jnp.where(live_rows, jnp.maximum(-gap[...], 0.0), 0.0)
-        squares = lanes_sum(depth * depth)
-        erecv[t, mine] = squares
-        to_all(erecv.at[t, mine], es_sem.at[t], er_sem.at[t])
-        for g in range(blocks // 8):
-            lo, hi = 8 * g, 8 * g + 8
-            terms = cat([depth[lo:hi] * geo[c, base + lo : base + hi] for c in range(3)])
-            top = terms.astype(bf16).astype(f32)
-            sums = mm(expand(cat([top, terms - top]), 8), hot[pl.ds(lo * pairs, 8 * pairs), :])
-            sums = sums[:24] + sums[24:]
-            for c in range(3):
-                wcat[lo:hi, c * bz : (c + 1) * bz] = sums[8 * c : 8 * c + 8]
-        parts = cat(split(wcat[...], 2))
+        erecv[t, mine] = lanes_sum(depth * depth)
+        to_all(erecv.at[t, mine], es_sem.at[slot], er_sem.at[slot])
+        own = scatter([depth * geo[c, base : base + blocks] for c in range(3)])
+        parts = cat(split(cat(own, 1), 2))
+        if t:
+            wait_all(erecv.at[t - 1], es_sem.at[1 - slot])
+            responded(t)
+            settle(scales[-1])
         if not last:
             far = apply(0, base, parts)
-            respond(
-                t + 1, lambda row, n: dots(row, n, [m[row : row + n] for m in far])
-            )
+            respond(t + 1, lambda row, n: dots(row, n, [m[row : row + n] for m in far]))
         moved = apply(base, blocks if last else 2 * blocks, parts)
-        near = jnp.concatenate([m[:blocks] for m in moved], axis=1)
+        near = cat([m[:blocks] for m in moved], 1)
+        near_ref[...] = near
         resid = jnp.sum(lanes_sum(near * near * first_col), axis=1, keepdims=True)
         rrecv[mine] = jnp.where(lane == t, resid, rrecv[mine])
         if last:
-            to_all(rrecv.at[mine], rs_sem, rr_sem)
+            to_all(rrecv.at[mine], es_sem.at[2], er_sem.at[2])
             for c in range(3):
                 cut = slice(c * bz, (c + 1) * bz)
                 done = placed(acc_ref[:, cut])
@@ -447,56 +536,32 @@
         else:
             step = dots(base, 2 * blocks, moved)
             step = step[:blocks] + step[blocks:]
-        others = erecv.at[t, pl.ds(0, devices - 1)]
-        pltpu.make_async_copy(others, others, er_sem.at[t]).wait()
+            more = received(t + 1)
+        wait_all(erecv.at[t], er_sem.at[slot])
         energy = jnp.sum(jnp.sum(erecv[t], axis=0), axis=1, keepdims=True)
         scale = 1.0 / (1.0 + energy / (blocks * pairs * devices))
-        hist_ref[0:1, :] = jnp.where(lane == t, energy, hist_ref[0:1, :])
-        hist_ref[1:2, :] = jnp.where(lane == t, scale, hist_ref[1:2, :])
+        energies.append(energy)
+        scales.append(scale)
         if last:
             for c in range(3):
                 out_ref[c] = out_ref[c] + scale[:, :, None] * step_ref[c]
         else:
-            acc_ref[...] = acc_ref[...] + (scale * first_col) * near
-            more = received(t + 1)
             gap[0:outer, :] = gap[0:outer, :] + scale * step[:outer]
             gap[pl.ds(outer, outer), :] = gap[pl.ds(outer, outer), :] + scale * (
                 step[outer:] + more
             )
 
-    rrecv[mine] = jnp.zeros((1, 128), f32)
-    hist_ref[...] = jnp.zeros_like(hist_ref)
-
-    def body(t, carry):
-        sweep(t, False)
-        return carry
-
-    lax.fori_loop(0, SWEEPS - 1, body, 0)
-    sweep(SWEEPS - 1, True)
-
-    for d, (axis, sign) in enumerate(dirs):
-
-        @pl.when(exists(axis, sign))
-        def _():
-            ask(d, axis, sign).wait_send()
-
-        @pl.when(exists(axis, -sign))
-        def _():
-            for t in range(SWEEPS):
-                answer(t, d, axis, sign).wait_send()
-
-    others = rrecv.at[pl.ds(0, devices - 1)]
-    pltpu.make_async_copy(others, others, rr_sem).wait()
+    wait_all(erecv.at[SWEEPS - 1], es_sem.at[(SWEEPS - 1) % 2])
+    energy, scale = jnp.zeros((1, 128), f32), jnp.zeros((1, 128), f32)
     for t in range(SWEEPS):
-        ref = erecv.at[t, pl.ds(0, devices - 1)]
-        pltpu.make_async_copy(ref, ref, es_sem.at[t]).wait()
-    others = rrecv.at[pl.ds(0, devices - 1)]
-    pltpu.make_async_copy(others, others, rs_sem).wait()
-    energy, scale = hist_ref[0:1, :], hist_ref[1:2, :]
-    resid = jnp.sum(rrecv[...], axis=0)
+        energy = jnp.where(lane == t, energies[t], energy)
+        scale = jnp.where(lane == t, scales[t], scale)
     hist_out[0:1, :] = jnp.sqrt(1.0 + energy / (blocks * pairs))[:, :SWEEPS]
-    resid = scale * scale * resid / (bx * by * bz)
+    factor = scale * scale / (bx * by * bz)
+    wait_all(rrecv, er_sem.at[2])
+    resid = factor * jnp.sum(rrecv[...], axis=0)
     hist_out[1:2, :] = jnp.sqrt(1.0 + resid)[:, :SWEEPS]
+    wait_all(rrecv, es_sem.at[2])
 
 
 def finish(pos_ref, hist_ref, pos_out, hist_out, sem):
@@ -516,6 +581,7 @@
     devices = sizes[0] * sizes[1] * sizes[2]
     outer = blocks // 2
     rows = 2 * blocks + 6 * outer
+    group = -(-3 * (blk[2] // 128) // 8) * 8
     dma = pltpu.SemaphoreType.DMA
     vmem = pl.BlockSpec(memory_space=pltpu.VMEM)
     moved, hist = pl.pallas_call(
@@ -535,11 +601,16 @@
             pltpu.VMEM(pair_geom.shape, f32),
             pltpu.VMEM(positions.shape, f32),
             pltpu.VMEM((blocks, 3 * blk[2]), f32),
-            pltpu.VMEM((8, 128), f32),
+            pltpu.VMEM((blocks, 3 * blk[2]), f32),
             pltpu.VMEM(positions.shape, f32),
-            pltpu.VMEM((4 * (pairs // 128) + 1, outer, 128), f32),
+            pltpu.VMEM((3, 3, blk[0] * blk[1], blk[2]), bf16),
+            pltpu.VMEM((outer, 128), f32),
+            pltpu.VMEM((6, outer, 128), f32),
+            pltpu.VMEM((6, 3, outer, blk[2]), f32),
+            pltpu.VMEM((6, 3, outer, blk[2]), f32),
+            pltpu.VMEM((4 * (pairs // 128), outer, 128), f32),
             pltpu.VMEM((2, blocks, pairs), f32),
-            pltpu.VMEM((blocks * pairs, blk[2]), bf16),
+            pltpu.VMEM((blocks * pairs, 128), bf16),
             pltpu.VMEM((1, 2 * blocks), f32),
             pltpu.VMEM((rows, 2 * blocks), bf16),
             pltpu.VMEM((rows, pairs), f32),
@@ -547,8 +618,9 @@
             pltpu.VMEM((rows, pairs), jnp.int32),
             pltpu.VMEM((rows, pairs), jnp.int32),
             pltpu.VMEM((blocks, pairs), f32),
-            pltpu.VMEM((blocks, 3 * blk[2]), f32),
-            pltpu.VMEM((6, 4 * (pairs // 128) + 1, outer, 128), f32),
+            pltpu.VMEM((pairs // 128, blocks * group, 128), f32),
+            pltpu.VMEM((blocks * group, 128), f32),
+            pltpu.VMEM((6, 4 * (pairs // 128), outer, 128), f32),
             pltpu.VMEM((SWEEPS, 6, outer, pairs), f32),
             pltpu.VMEM((SWEEPS, 6, outer, pairs), f32),
             pltpu.VMEM((SWEEPS, devices, 1, 128), f32),
@@ -556,14 +628,10 @@
             dma((6,)),
             pltpu.SemaphoreType.REGULAR((len(near_radii(sizes)),)),
             pltpu.SemaphoreType.REGULAR,
-            dma((6,)),
-            dma((6,)),
-            dma((SWEEPS, 6)),
-            dma((SWEEPS, 6)),
-            dma((SWEEPS,)),
-            dma((SWEEPS,)),
-            dma,
-            dma,
+            dma((4, 6)),
+            dma((4, 6)),
+            dma((3,)),
+            dma((3,)),
         ],
         compiler_params=pltpu.CompilerParams(
             collective_id=0, has_side_effects=True, vmem_limit_bytes=40 << 20

time: 41.2 us -> 39 us (0.947)
  Pallas kernels: 39.7 us -> 37.6 us
    pallas_call x1, Pallas kernels: 38.8 us -> 36.7 us  [local(): pl.pallas_call(functools.partial(kernel, sizes, blk), out_shape=(pltpu.VM...]
where the time goes in v3:
time: 39 us; the launch traced here: 38.9 us
  Pallas kernels  37.6 us (96%)
  between operations  1.29 us (3%)
    pallas_call x1, Pallas kernels, local(): pl.pallas_call(functools.partial(kernel, sizes, blk), out_shape=(pltpu.VM...  36.7 us
    pallas_call x1, Pallas kernels, local(): pl.pallas_call(finish, out_shape=(jax.ShapeDtypeStruct(positions.shape, f...  0.9 us

profile of v3, /device:TPU:0, one launch (start us, length us, event | category | flops | bytes accessed | tf_op | source)
XLA Modules:
  0.0 38.9 jit_solution(886086396886406125)
XLA Ops:
  1.3 36.7 %shard_map.86 = (f32[3,16,16,256]{3,2,1,0:T(8,128)S(1)}, f32[2,5]{1,0:T(2,128)S(1)}) custom-call(s32[1,1,1]{2,1,0:T(1,128)S(6)} %copy.9.live_ref, s32[1,1,1,32,256]{4,3,2,1,0:T(8,128)} %node_hbm.1, s32[1,1,1,32]{3,2,1,0:T(1,128)} %line_hbm.1, s32[1,1,1,32,256]{4,3,2,1,0:T(8,128)} %farpos_hbm.1, s32[1,1,1,32]{3,2,1,0:T(1,128)} %farline_hbm.1, ...), custom_call_target="tpu_custom_call" | custom-call | tf_op jit(solution)/shard_map/pallas_call | solution.py:587
  38.0 0.9 %shard_map.87 = (f32[3,16,16,256]{3,2,1,0:T(8,128)}, f32[2,5]{1,0:T(2,128)}) custom-call(f32[3,16,16,256]{3,2,1,0:T(8,128)S(1)} %get-tuple-element.4.pos_ref, f32[2,5]{1,0:T(2,128)S(1)} %get-tuple-element.5.hist_ref), custom_call_target="tpu_custom_call" | custom-call | tf_op jit(solution)/shard_map/pallas_call | solution.py:653

commit v4 on v3

--- a/solution.py
+++ b/solution.py
@@ -79,6 +79,7 @@
     pos3,
     code,
     codes,
+    there,
     lsend,
     lrecv,
     req,
@@ -98,7 +99,6 @@
     drecv,
     erecv,
     rrecv,
-    in_sem,
     near_sem,
     whole_sem,
     ds_sem,
@@ -162,17 +162,15 @@
     barrier = pltpu.get_barrier_semaphore()
     signal_sphere(barrier, 1)
     inputs = [
-        pltpu.make_async_copy(src, dst, in_sem.at[i])
-        for i, (src, dst) in enumerate(
-            [
-                (farline_hbm, farline_ref),
-                (farpos_hbm, farpos_ref),
-                (geom_hbm, geom_ref),
-                (node_hbm, node_ref),
-                (line_hbm, line_ref),
-                (pos_hbm, pos_ref),
-            ]
-        )
+        pltpu.make_async_copy(*copy)
+        for copy in [
+            (farline_hbm, farline_ref, ds_sem.at[0, 0]),
+            (farpos_hbm, farpos_ref, ds_sem.at[0, 1]),
+            (geom_hbm, geom_ref, ds_sem.at[0, 2]),
+            (node_hbm, node_ref, es_sem.at[0]),
+            (line_hbm, line_ref, es_sem.at[1]),
+            (pos_hbm, pos_ref, es_sem.at[2]),
+        ]
     ]
     for copy in inputs:
         copy.start()
@@ -190,48 +188,72 @@
         for h in range(wide):
             req[c * wide + h] = planes[c][:, 128 * h : 128 * (h + 1)]
     cols[1] = column(farline_ref)
-    code[...] = cols[1, outer:, :128]
-
-    def remote(src, dst, slot, d, to):
+    row = farline_ref[0, 0].astype(f32)
+    code[...] = jnp.concatenate([row] * (128 // blocks), axis=1)
+
+    def remote(src, dst, send_sem, recv_sem, to):
         return pltpu.make_async_remote_copy(
             src_ref=src,
             dst_ref=dst,
-            send_sem=ds_sem.at[slot, d],
-            recv_sem=dr_sem.at[slot, d],
+            send_sem=send_sem,
+            recv_sem=recv_sem,
             device_id=neighbour(*to),
             device_id_type=MESH,
         )
 
     def ask_line(d, axis, sign):
-        return remote(code, codes.at[d], 2, d, (axis, sign))
+        return remote(code, codes.at[pl.ds(d, 1), :], ds_sem.at[1, d], dr_sem.at[1, d], (axis, sign))
 
     def ask_pairs(d, axis, sign):
-        return remote(req, reqs.at[d], 3, d, (axis, sign))
+        return remote(req, reqs.at[d], ds_sem.at[0, d], dr_sem.at[2, d], (axis, sign))
 
     def line_back(d, axis, sign):
-        return remote(lsend.at[d], lrecv.at[d], 0, d, (axis, -sign))
+        sems = ds_sem.at[1, d], dr_sem.at[0, d]
+        return remote(lsend.at[d], lrecv.at[d], *sems, (axis, -sign))
 
     def answer(t, d, axis, sign):
-        return remote(dsend.at[t, d], drecv.at[t, d], t % 2, d, (axis, -sign))
+        sems = ds_sem.at[t % 2, d], dr_sem.at[t % 2, d]
+        return remote(dsend.at[t, d], drecv.at[t, d], *sems, (axis, -sign))
+
+    def first_side(side):
+        odd = lax.rem(me[1], 2) == 1
+        return odd if side > 0 else jnp.logical_not(odd)
+
+    def start_two(copy, way):
+        for first in (True, False):
+            for d in range(2):
+                axis, sign = dirs[d]
+                turn = first_side(way * sign)
+                turn = turn if first else jnp.logical_not(turn)
+
+                @pl.when(exists(axis, way * sign) & turn)
+                def _():
+                    copy(d, axis, sign).start()
+
+    def start_rest(copy, way, d):
+        axis, sign = dirs[d]
+
+        @pl.when(exists(axis, way * sign))
+        def _():
+            copy(d, axis, sign).start()
 
     wait_sphere(barrier, 1)
     for ask in (ask_line, ask_pairs):
-        for d, (axis, sign) in enumerate(dirs):
-
-            @pl.when(exists(axis, sign))
-            def _():
-                ask(d, axis, sign).start()
+        start_two(ask, 1)
+        for d in range(2, len(dirs)):
+            start_rest(ask, 1, d)
 
     signal_sphere(near_sem.at[0], radii[0])
     for copy in inputs[3:5]:
         copy.wait()
     cols[0] = column(line_ref)
 
+    codes[len(dirs) :] = jnp.zeros((8 - len(dirs), 128), f32)
     for d, (axis, sign) in enumerate(dirs):
 
         @pl.when(jnp.logical_not(exists(axis, -sign)))
         def _():
-            codes[d] = jnp.zeros(code.shape, f32)
+            codes[pl.ds(d, 1), :] = jnp.zeros(code.shape, f32)
             reqs[d] = jnp.zeros(req.shape, f32)
 
         @pl.when(jnp.logical_not(exists(axis, sign)))
@@ -344,18 +366,24 @@
     shifts = []
     for axis, sign in dirs:
         shifts.append([sign if a == axis else 0 for a in range(3)])
+    turned = jnp.transpose(codes[...])[outer:blocks]
     asked = []
     for d in range(len(dirs)):
-        there = jnp.concatenate([codes[d]] * wide, axis=1)
-        asked.append(located(there, 0.0, shifts[d])[0])
+        there[d] = jnp.broadcast_to(turned[:, d : d + 1], (outer, pairs))
+        asked.append(located(there[d], 0.0, shifts[d])[0])
     back = fetch(cat(asked))
-    for d, (axis, sign) in enumerate(dirs):
+    for d in range(len(dirs)):
         for c in range(3):
             lsend[d, c] = back[c][d * outer : (d + 1) * outer]
-
-        @pl.when(exists(axis, -sign))
-        def _():
-            line_back(d, axis, sign).start()
+    for d, (axis, sign) in enumerate(dirs):
+
+        @pl.when(exists(axis, sign))
+        def _():
+            ask_line(d, axis, sign).wait_send()
+
+    start_two(line_back, -1)
+    for d in range(2, len(dirs)):
+        start_rest(line_back, -1, d)
 
     for i, r in enumerate(radii[1:], 1):
         wait_sphere(near_sem.at[i], r)
@@ -381,8 +409,7 @@
         got = [
             jnp.concatenate([reqs[d, c * wide + h] for h in range(wide)], axis=1) for c in range(4)
         ]
-        there = jnp.concatenate([codes[d]] * wide, axis=1)
-        _, at, ok = located(there, got[3], shifts[d])
+        _, at, ok = located(there[d], got[3], shifts[d])
         pairs_in.append([jnp.where(ok, at, 0.0)] + [jnp.where(ok, -got[c], 0.0) for c in range(3)])
     pairs_in = [cat([x[i] for x in pairs_in]) for i in range(4)]
     setup(0, cat(asked), pairs_in[0], pairs_in[1:])
@@ -413,7 +440,6 @@
 
         @pl.when(exists(axis, sign))
         def _():
-            ask_line(d, axis, sign).wait_send()
             ask_pairs(d, axis, sign).wait_send()
 
         @pl.when(exists(axis, -sign))
@@ -421,12 +447,13 @@
             line_back(d, axis, sign).wait_send()
 
     def respond(t, total):
-        for d, (axis, sign) in enumerate(dirs):
+        send = functools.partial(answer, t)
+        for d in range(len(dirs)):
             dsend[t, d] = total(d * outer, outer)
-
-            @pl.when(exists(axis, -sign))
-            def _():
-                answer(t, d, axis, sign).start()
+            if d == 1:
+                start_two(send, -1)
+            if d > 1:
+                start_rest(send, -1, d)
 
     def responded(t):
         for d, (axis, sign) in enumerate(dirs):
@@ -604,8 +631,9 @@
             pltpu.VMEM((blocks, 3 * blk[2]), f32),
             pltpu.VMEM(positions.shape, f32),
             pltpu.VMEM((3, 3, blk[0] * blk[1], blk[2]), bf16),
-            pltpu.VMEM((outer, 128), f32),
-            pltpu.VMEM((6, outer, 128), f32),
+            pltpu.VMEM((1, 128), f32),
+            pltpu.VMEM((8, 128), f32),
+            pltpu.VMEM((6, outer, pairs), f32),
             pltpu.VMEM((6, 3, outer, blk[2]), f32),
             pltpu.VMEM((6, 3, outer, blk[2]), f32),
             pltpu.VMEM((4 * (pairs // 128), outer, 128), f32),
@@ -625,11 +653,10 @@
             pltpu.VMEM((SWEEPS, 6, outer, pairs), f32),
             pltpu.VMEM((SWEEPS, devices, 1, 128), f32),
             pltpu.VMEM((devices, 1, 128), f32),
-            dma((6,)),
             pltpu.SemaphoreType.REGULAR((len(near_radii(sizes)),)),
             pltpu.SemaphoreType.REGULAR,
-            dma((4, 6)),
-            dma((4, 6)),
+            dma((2, 6)),
+            dma((3, 6)),
             dma((3,)),
             dma((3,)),
         ],

time: 39 us -> 38.7 us (level)
  Pallas kernels: 37.6 us -> 37.2 us
where the time goes in v4:
time: 38.7 us; the launch traced here: 38.5 us
  Pallas kernels  37.2 us (96%)
  between operations  1.29 us (3%)
    pallas_call x1, Pallas kernels, local(): pl.pallas_call(functools.partial(kernel, sizes, blk), out_shape=(pltpu.VM...  36.3 us
    pallas_call x1, Pallas kernels, local(): pl.pallas_call(finish, out_shape=(jax.ShapeDtypeStruct(positions.shape, f...  0.9 us

profile of v4, /device:TPU:0, one launch (start us, length us, event | category | flops | bytes accessed | tf_op | source)
XLA Modules:
  0.0 38.5 jit_solution(18160882370218003742)
XLA Ops:
  1.3 36.3 %shard_map.86 = (f32[3,16,16,256]{3,2,1,0:T(8,128)S(1)}, f32[2,5]{1,0:T(2,128)S(1)}) custom-call(s32[1,1,1]{2,1,0:T(1,128)S(6)} %copy.9.live_ref, s32[1,1,1,32,256]{4,3,2,1,0:T(8,128)} %node_hbm.1, s32[1,1,1,32]{3,2,1,0:T(1,128)} %line_hbm.1, s32[1,1,1,32,256]{4,3,2,1,0:T(8,128)} %farpos_hbm.1, s32[1,1,1,32]{3,2,1,0:T(1,128)} %farline_hbm.1, ...), custom_call_target="tpu_custom_call" | custom-call | tf_op jit(solution)/shard_map/pallas_call | solution.py:614
  37.6 0.9 %shard_map.87 = (f32[3,16,16,256]{3,2,1,0:T(8,128)}, f32[2,5]{1,0:T(2,128)}) custom-call(f32[3,16,16,256]{3,2,1,0:T(8,128)S(1)} %get-tuple-element.4.pos_ref, f32[2,5]{1,0:T(2,128)S(1)} %get-tuple-element.5.hist_ref), custom_call_target="tpu_custom_call" | custom-call | tf_op jit(solution)/shard_map/pallas_call | solution.py:680

commit v5 on v4

--- a/solution.py
+++ b/solution.py
@@ -129,8 +129,10 @@
         return (to // (ny * nz), lax.rem(to // nz, ny), lax.rem(to, nz))
 
     def moved_by(axis, k):
+        if sizes[axis] & (sizes[axis] - 1) == 0:
+            return lax.bitwise_xor(me[axis], k)
         to = me[axis] + k
-        return jnp.where(to >= sizes[axis], to - sizes[axis], to) if k else to
+        return jnp.where(to >= sizes[axis], to - sizes[axis], to)
 
     ids = [[moved_by(a, k) for k in range(sizes[a])] for a in range(3)]
 
@@ -164,12 +166,12 @@
     inputs = [
         pltpu.make_async_copy(*copy)
         for copy in [
-            (farline_hbm, farline_ref, ds_sem.at[0, 0]),
-            (farpos_hbm, farpos_ref, ds_sem.at[0, 1]),
-            (geom_hbm, geom_ref, ds_sem.at[0, 2]),
-            (node_hbm, node_ref, es_sem.at[0]),
-            (line_hbm, line_ref, es_sem.at[1]),
-            (pos_hbm, pos_ref, es_sem.at[2]),
+            (farline_hbm, farline_ref, ds_sem.at[0]),
+            (farpos_hbm, farpos_ref, ds_sem.at[1]),
+            (geom_hbm, geom_ref, es_sem.at[0]),
+            (node_hbm, node_ref, es_sem.at[1]),
+            (line_hbm, line_ref, es_sem.at[2]),
+            (pos_hbm, pos_ref, ds_sem.at[2]),
         ]
     ]
     for copy in inputs:
@@ -202,18 +204,27 @@
         )
 
     def ask_line(d, axis, sign):
-        return remote(code, codes.at[pl.ds(d, 1), :], ds_sem.at[1, d], dr_sem.at[1, d], (axis, sign))
+        return remote(code, codes.at[pl.ds(d, 1), :], ds_sem.at[1], dr_sem.at[1], (axis, sign))
 
     def ask_pairs(d, axis, sign):
-        return remote(req, reqs.at[d], ds_sem.at[0, d], dr_sem.at[2, d], (axis, sign))
+        return remote(req, reqs.at[d], ds_sem.at[0], dr_sem.at[2], (axis, sign))
 
     def line_back(d, axis, sign):
-        sems = ds_sem.at[1, d], dr_sem.at[0, d]
-        return remote(lsend.at[d], lrecv.at[d], *sems, (axis, -sign))
+        return remote(lsend.at[d], lrecv.at[d], ds_sem.at[1], dr_sem.at[0], (axis, -sign))
 
     def answer(t, d, axis, sign):
-        sems = ds_sem.at[t % 2, d], dr_sem.at[t % 2, d]
+        sems = ds_sem.at[t % 2], dr_sem.at[t % 2]
         return remote(dsend.at[t, d], drecv.at[t, d], *sems, (axis, -sign))
+
+    count = sum(jnp.where(exists(axis, sign), 1, 0) for axis, sign in dirs)
+
+    def wait_each(ref, sem):
+        for k in range(1, len(dirs) + 1):
+
+            @pl.when(count == k)
+            def _():
+                some = ref.at[pl.ds(0, k)]
+                pltpu.make_async_copy(some, some, sem).wait()
 
     def first_side(side):
         odd = lax.rem(me[1], 2) == 1
@@ -357,12 +368,7 @@
             pos3[c, k] = part
     vals = fetch(cat([line_b, line]))
 
-    for d, (axis, sign) in enumerate(dirs):
-
-        @pl.when(exists(axis, -sign))
-        def _():
-            ask_line(d, axis, sign).wait_recv()
-
+    wait_each(codes, dr_sem.at[1])
     shifts = []
     for axis, sign in dirs:
         shifts.append([sign if a == axis else 0 for a in range(3)])
@@ -375,12 +381,7 @@
     for d in range(len(dirs)):
         for c in range(3):
             lsend[d, c] = back[c][d * outer : (d + 1) * outer]
-    for d, (axis, sign) in enumerate(dirs):
-
-        @pl.when(exists(axis, sign))
-        def _():
-            ask_line(d, axis, sign).wait_send()
-
+    wait_each(codes, ds_sem.at[1])
     start_two(line_back, -1)
     for d in range(2, len(dirs)):
         start_rest(line_back, -1, d)
@@ -398,12 +399,7 @@
     gap[...] = sum(geom[c] * start[c] for c in range(3)) - geom[3]
     gap[0:outer, :] = gap[0:outer, :] - sum(geom[c][:outer] * inner[c] for c in range(3))
 
-    for d, (axis, sign) in enumerate(dirs):
-
-        @pl.when(exists(axis, -sign))
-        def _():
-            ask_pairs(d, axis, sign).wait_recv()
-
+    wait_each(reqs, dr_sem.at[2])
     pairs_in = []
     for d in range(len(dirs)):
         got = [
@@ -414,12 +410,7 @@
     pairs_in = [cat([x[i] for x in pairs_in]) for i in range(4)]
     setup(0, cat(asked), pairs_in[0], pairs_in[1:])
 
-    for d, (axis, sign) in enumerate(dirs):
-
-        @pl.when(exists(axis, sign))
-        def _():
-            line_back(d, axis, sign).wait_recv()
-
+    wait_each(lrecv, dr_sem.at[0])
     low, half = at_lanes(far[outer:] - RIM)
     reach = []
     for c in range(3):
@@ -436,16 +427,6 @@
     gap[pl.ds(outer, outer), :] = gap[pl.ds(outer, outer), :] - sum(
         geom[c][outer:] * reach[c] for c in range(3)
     )
-    for d, (axis, sign) in enumerate(dirs):
-
-        @pl.when(exists(axis, sign))
-        def _():
-            ask_pairs(d, axis, sign).wait_send()
-
-        @pl.when(exists(axis, -sign))
-        def _():
-            line_back(d, axis, sign).wait_send()
-
     def respond(t, total):
         send = functools.partial(answer, t)
         for d in range(len(dirs)):
@@ -456,19 +437,10 @@
                 start_rest(send, -1, d)
 
     def responded(t):
-        for d, (axis, sign) in enumerate(dirs):
-
-            @pl.when(exists(axis, -sign))
-            def _():
-                answer(t, d, axis, sign).wait_send()
+        wait_each(dsend.at[t], ds_sem.at[t % 2])
 
     def received(t):
-        for d, (axis, sign) in enumerate(dirs):
-
-            @pl.when(exists(axis, sign))
-            def _():
-                answer(t, d, axis, sign).wait_recv()
-
+        wait_each(drecv.at[t], dr_sem.at[t % 2])
         got = drecv[t, 0]
         for d in range(1, len(dirs)):
             got = got + drecv[t, d]
@@ -488,8 +460,8 @@
             ).start()
 
         if devices <= 32:
-            for a in range(nx):
-                for b in range(ny):
+            for a in reversed(range(nx)):
+                for b in reversed(range(ny)):
                     for c in range(nz):
                         if a or b or c:
                             send((ids[0][a], ids[1][b], ids[2][c]))
@@ -541,20 +513,25 @@
         to_all(erecv.at[t, mine], es_sem.at[slot], er_sem.at[slot])
         own = scatter([depth * geo[c, base : base + blocks] for c in range(3)])
         parts = cat(split(cat(own, 1), 2))
-        if t:
-            wait_all(erecv.at[t - 1], es_sem.at[1 - slot])
-            responded(t)
-            settle(scales[-1])
+        if not t:
+            wait_each(lrecv, ds_sem.at[1])
         if not last:
             far = apply(0, base, parts)
             respond(t + 1, lambda row, n: dots(row, n, [m[row : row + n] for m in far]))
         moved = apply(base, blocks if last else 2 * blocks, parts)
         near = cat([m[:blocks] for m in moved], 1)
-        near_ref[...] = near
         resid = jnp.sum(lanes_sum(near * near * first_col), axis=1, keepdims=True)
         rrecv[mine] = jnp.where(lane == t, resid, rrecv[mine])
         if last:
             to_all(rrecv.at[mine], es_sem.at[2], er_sem.at[2])
+        if t:
+            wait_all(erecv.at[t - 1], es_sem.at[1 - slot])
+            responded(t)
+            settle(scales[-1])
+        else:
+            wait_each(reqs, ds_sem.at[0])
+        near_ref[...] = near
+        if last:
             for c in range(3):
                 cut = slice(c * bz, (c + 1) * bz)
                 done = placed(acc_ref[:, cut])
@@ -655,8 +632,8 @@
             pltpu.VMEM((devices, 1, 128), f32),
             pltpu.SemaphoreType.REGULAR((len(near_radii(sizes)),)),
             pltpu.SemaphoreType.REGULAR,
-            dma((2, 6)),
-            dma((3, 6)),
+            dma((3,)),
+            dma((3,)),
             dma((3,)),
             dma((3,)),
         ],

time: 38.7 us -> 38 us (0.982)
  Pallas kernels: 37.2 us -> 36.5 us
    pallas_call x1, Pallas kernels: 36.3 us -> 35.6 us  [local(): pl.pallas_call(functools.partial(kernel, sizes, blk), out_shape=(pltpu.VM...]
where the time goes in v5:
time: 38 us; the launch traced here: 37.8 us
  Pallas kernels  36.5 us (96%)
  between operations  1.29 us (3%)
    pallas_call x1, Pallas kernels, local(): pl.pallas_call(functools.partial(kernel, sizes, blk), out_shape=(pltpu.VM...  35.6 us
    pallas_call x1, Pallas kernels, local(): pl.pallas_call(finish, out_shape=(jax.ShapeDtypeStruct(positions.shape, f...  0.9 us

profile of v5, /device:TPU:0, one launch (start us, length us, event | category | flops | bytes accessed | tf_op | source)
XLA Modules:
  0.0 37.8 jit_solution(12996893815407790839)
XLA Ops:
  1.3 35.6 %shard_map.86 = (f32[3,16,16,256]{3,2,1,0:T(8,128)S(1)}, f32[2,5]{1,0:T(2,128)S(1)}) custom-call(s32[1,1,1]{2,1,0:T(1,128)S(6)} %copy.9.live_ref, s32[1,1,1,32,256]{4,3,2,1,0:T(8,128)} %node_hbm.1, s32[1,1,1,32]{3,2,1,0:T(1,128)} %line_hbm.1, s32[1,1,1,32,256]{4,3,2,1,0:T(8,128)} %farpos_hbm.1, s32[1,1,1,32]{3,2,1,0:T(1,128)} %farline_hbm.1, ...), custom_call_target="tpu_custom_call" | custom-call | tf_op jit(solution)/shard_map/pallas_call | solution.py:591
  36.9 0.9 %shard_map.87 = (f32[3,16,16,256]{3,2,1,0:T(8,128)}, f32[2,5]{1,0:T(2,128)}) custom-call(f32[3,16,16,256]{3,2,1,0:T(8,128)S(1)} %get-tuple-element.4.pos_ref, f32[2,5]{1,0:T(2,128)S(1)} %get-tuple-element.5.hist_ref), custom_call_target="tpu_custom_call" | custom-call | tf_op jit(solution)/shard_map/pallas_call | solution.py:657

commit v6 on v5

--- a/solution.py
+++ b/solution.py
@@ -62,7 +62,7 @@
     node_hbm,
     line_hbm,
     farpos_hbm,
-    farline_hbm,
+    farline_ref,
     geom_hbm,
     pos_hbm,
     out_ref,
@@ -70,7 +70,6 @@
     node_ref,
     line_ref,
     farpos_ref,
-    farline_ref,
     geom_ref,
     pos_ref,
     acc_ref,
@@ -166,8 +165,7 @@
     inputs = [
         pltpu.make_async_copy(*copy)
         for copy in [
-            (farline_hbm, farline_ref, ds_sem.at[0]),
-            (farpos_hbm, farpos_ref, ds_sem.at[1]),
+            (farpos_hbm, farpos_ref, ds_sem.at[0]),
             (geom_hbm, geom_ref, es_sem.at[0]),
             (node_hbm, node_ref, es_sem.at[1]),
             (line_hbm, line_ref, es_sem.at[2]),
@@ -176,20 +174,10 @@
     ]
     for copy in inputs:
         copy.start()
-    for copy in inputs[:3]:
-        copy.wait()
-
     def column(ref):
         row = ref[0, 0].astype(f32)
         return jnp.transpose(jnp.broadcast_to(row, (pairs, blocks)))
 
-    wide = pairs // 128
-    planes = [geom_ref[0, 0, 0, outer:, c, :] for c in range(3)]
-    planes.append(farpos_ref[0, 0, 0, outer:, :].astype(f32))
-    for c in range(4):
-        for h in range(wide):
-            req[c * wide + h] = planes[c][:, 128 * h : 128 * (h + 1)]
-    cols[1] = column(farline_ref)
     row = farline_ref[0, 0].astype(f32)
     code[...] = jnp.concatenate([row] * (128 // blocks), axis=1)
 
@@ -249,15 +237,26 @@
             copy(d, axis, sign).start()
 
     wait_sphere(barrier, 1)
-    for ask in (ask_line, ask_pairs):
-        start_two(ask, 1)
-        for d in range(2, len(dirs)):
-            start_rest(ask, 1, d)
+    start_two(ask_line, 1)
+    for d in range(2, len(dirs)):
+        start_rest(ask_line, 1, d)
+    for copy in inputs[:2]:
+        copy.wait()
+    wide = pairs // 128
+    planes = [geom_ref[0, 0, 0, outer:, c, :] for c in range(3)]
+    planes.append(farpos_ref[0, 0, 0, outer:, :].astype(f32))
+    for c in range(4):
+        for h in range(wide):
+            req[c * wide + h] = planes[c][:, 128 * h : 128 * (h + 1)]
+    start_two(ask_pairs, 1)
+    for d in range(2, len(dirs)):
+        start_rest(ask_pairs, 1, d)
 
     signal_sphere(near_sem.at[0], radii[0])
-    for copy in inputs[3:5]:
+    for copy in inputs[2:4]:
         copy.wait()
     cols[0] = column(line_ref)
+    cols[1] = column(farline_ref)
 
     codes[len(dirs) :] = jnp.zeros((8 - len(dirs), 128), f32)
     for d, (axis, sign) in enumerate(dirs):
@@ -283,14 +282,21 @@
     node_t = jnp.transpose(node_low.astype(f32))
     group = terms.shape[1] // blocks
     terms[...] = jnp.zeros_like(terms)
-    for b in range(blocks):
-        if b == outer:
-            wait_sphere(near_sem.at[0], radii[0])
-            if len(radii) > 1:
-                signal_sphere(near_sem.at[1], radii[1])
-        hot[pl.ds(b * pairs, pairs), :] = jnp.where(
-            node_t[:, b : b + 1] == lane_node, 1.0, 0.0
-        ).astype(bf16)
+
+    def mark(slots):
+        for b in slots:
+            hot[pl.ds(b * pairs, pairs), :] = jnp.where(
+                node_t[:, b : b + 1] == lane_node, 1.0, 0.0
+            ).astype(bf16)
+
+    mark(range(outer))
+    wait_sphere(near_sem.at[0], radii[0])
+    if len(radii) > 1:
+        signal_sphere(near_sem.at[1], radii[1])
+    inputs[4].wait()
+    for c in range(3):
+        for k, part in enumerate(split(pos_ref[c].reshape(lines, bz), 3)):
+            pos3[c, k] = part
     row_line = line_ref[0, 0].astype(f32)
     two[...] = jnp.concatenate([row_line, row_line], axis=1)
     row_mod = lax.broadcasted_iota(jnp.int32, (blocks, blocks), 0)
@@ -322,9 +328,6 @@
             for c in range(n)
         ]
 
-    ones = jnp.where(live_rows, 1.0, 0.0)
-    counts = scatter([ones, jnp.zeros_like(ones), jnp.zeros_like(ones)])[0].astype(bf16)
-
     def located(code, zpos, shift):
         e = jnp.floor((code + 0.5) / (by + 2 * RIM))
         f = code - e * (by + 2 * RIM)
@@ -355,19 +358,6 @@
     node = node_ref[0, 0, 0].astype(f32)
     far = farpos_ref[0, 0, 0].astype(f32)
     geom = [geom_ref[0, 0, 0, :, c, :] for c in range(4)]
-    line, z, ok = located(cols[1], far, (0, 0, 0))
-    setup(
-        base,
-        cat([line_b, line]),
-        cat([node, jnp.where(ok, z, 0.0)]),
-        [cat([geom[c], jnp.where(ok, -geom[c], 0.0)]) for c in range(3)],
-    )
-    inputs[5].wait()
-    for c in range(3):
-        for k, part in enumerate(split(pos_ref[c].reshape(lines, bz), 3)):
-            pos3[c, k] = part
-    vals = fetch(cat([line_b, line]))
-
     wait_each(codes, dr_sem.at[1])
     shifts = []
     for axis, sign in dirs:
@@ -394,6 +384,17 @@
         to = (ids[0][k], me[1], me[2])
         pl.semaphore_signal(whole_sem, inc=1, device_id=to, device_id_type=MESH)
 
+    mark(range(outer, blocks))
+    ones = jnp.where(live_rows, 1.0, 0.0)
+    counts = scatter([ones, jnp.zeros_like(ones), jnp.zeros_like(ones)])[0].astype(bf16)
+    line, z, ok = located(cols[1], far, (0, 0, 0))
+    setup(
+        base,
+        cat([line_b, line]),
+        cat([node, jnp.where(ok, z, 0.0)]),
+        [cat([geom[c], jnp.where(ok, -geom[c], 0.0)]) for c in range(3)],
+    )
+    vals = fetch(cat([line_b, line]))
     start = take_lanes([v[:blocks] for v in vals], *at_lanes(node))
     inner = take_lanes([v[blocks : blocks + outer] for v in vals], *at_lanes(z[:outer]))
     gap[...] = sum(geom[c] * start[c] for c in range(3)) - geom[3]
@@ -588,6 +589,7 @@
     group = -(-3 * (blk[2] // 128) // 8) * 8
     dma = pltpu.SemaphoreType.DMA
     vmem = pl.BlockSpec(memory_space=pltpu.VMEM)
+    hbm = functools.partial(pltpu.with_memory_space_constraint, memory_space=pltpu.HBM)
     moved, hist = pl.pallas_call(
         functools.partial(kernel, sizes, blk),
         out_shape=(
@@ -595,13 +597,14 @@
             pltpu.VMEM((2, SWEEPS), f32),
         ),
         in_specs=[pl.BlockSpec(memory_space=pltpu.SMEM)]
-        + [pl.BlockSpec(memory_space=pltpu.HBM)] * 6,
+        + [pl.BlockSpec(memory_space=pltpu.HBM)] * 3
+        + [vmem]
+        + [pl.BlockSpec(memory_space=pltpu.HBM)] * 2,
         out_specs=(vmem, vmem),
         scratch_shapes=[
             pltpu.VMEM(pair_node.shape, jnp.int32),
             pltpu.VMEM(pair_line.shape, jnp.int32),
             pltpu.VMEM(pair_far.shape, jnp.int32),
-            pltpu.VMEM(far_line.shape, jnp.int32),
             pltpu.VMEM(pair_geom.shape, f32),
             pltpu.VMEM(positions.shape, f32),
             pltpu.VMEM((blocks, 3 * blk[2]), f32),
@@ -642,17 +645,12 @@
         ),
     )(
         live_blocks,
-        *[
-            pltpu.with_memory_space_constraint(x, pltpu.HBM)
-            for x in (
-                pair_node,
-                pair_line,
-                pair_far,
-                far_line,
-                pair_geom,
-                positions,
-            )
-        ]
+        hbm(pair_node),
+        hbm(pair_line),
+        hbm(pair_far),
+        pltpu.with_memory_space_constraint(far_line, pltpu.VMEM),
+        hbm(pair_geom),
+        hbm(positions),
     )
     return pl.pallas_call(
         finish,

time: 38 us -> 38 us (level)
  no operation moved by 1% of the time
where the time goes in v6:
time: 38 us; the launch traced here: 37.8 us
  Pallas kernels  36.5 us (96%)
  between operations  1.31 us (3%)
    pallas_call x1, Pallas kernels, local(): pl.pallas_call(functools.partial(kernel, sizes, blk), out_shape=(pltpu.VM...  35.6 us
    pallas_call x1, Pallas kernels, local(): pl.pallas_call(finish, out_shape=(jax.ShapeDtypeStruct(positions.shape, f...  0.9 us

profile of v6, /device:TPU:0, one launch (start us, length us, event | category | flops | bytes accessed | tf_op | source)
XLA Modules:
  0.0 37.8 jit_solution(8418993021911746726)
XLA Ops:
  0.6 0.0 copy-start
  1.3 0.0 copy-done
  1.3 35.6 %shard_map.86 = (f32[3,16,16,256]{3,2,1,0:T(8,128)S(1)}, f32[2,5]{1,0:T(2,128)S(1)}) custom-call(s32[1,1,1]{2,1,0:T(1,128)S(6)} %copy.9.live_ref, s32[1,1,1,32,256]{4,3,2,1,0:T(8,128)} %node_hbm.1, s32[1,1,1,32]{3,2,1,0:T(1,128)} %line_hbm.1, s32[1,1,1,32,256]{4,3,2,1,0:T(8,128)} %farpos_hbm.1, s32[1,1,1,32]{3,2,1,0:T(1,128)S(1)} %copy-done, ...), custom_call_target="tpu_custom_call" | custom-call | tf_op jit(solution)/shard_map/pallas_call | solution.py:593
  36.9 0.9 %shard_map.87 = (f32[3,16,16,256]{3,2,1,0:T(8,128)}, f32[2,5]{1,0:T(2,128)}) custom-call(f32[3,16,16,256]{3,2,1,0:T(8,128)S(1)} %get-tuple-element.4.pos_ref, f32[2,5]{1,0:T(2,128)S(1)} %get-tuple-element.5.hist_ref), custom_call_target="tpu_custom_call" | custom-call | tf_op jit(solution)/shard_map/pallas_call | solution.py:655
Async XLA Ops:
  0.6 0.7 %copy-start = (s32[1,1,1,32]{3,2,1,0:T(1,128)S(1)}, s32[1,1,1,32]{3,2,1,0:T(1,128)}, u32[]{:S(2)}) copy-start(s32[1,1,1,32]{3,2,1,0:T(1,128)} %farline_ref.1) | copy-start | bytes 388

commit v7 on v6

--- a/solution.py
+++ b/solution.py
@@ -78,7 +78,6 @@
     pos3,
     code,
     codes,
-    there,
     lsend,
     lrecv,
     req,
@@ -137,7 +136,8 @@
 
     def sphere(r):
         steps = itertools.product(*[range(1 - n, n) for n in sizes])
-        return [s for s in steps if sum(abs(x) for x in s) == r]
+        steps = [s for s in steps if sum(abs(x) for x in s) == r]
+        return sorted(steps, key=lambda s: -abs(s[1]))
 
     def inside(step):
         ok = True
@@ -178,8 +178,8 @@
         row = ref[0, 0].astype(f32)
         return jnp.transpose(jnp.broadcast_to(row, (pairs, blocks)))
 
-    row = farline_ref[0, 0].astype(f32)
-    code[...] = jnp.concatenate([row] * (128 // blocks), axis=1)
+    cols[1] = column(farline_ref)
+    code[...] = cols[1, outer:, :128]
 
     def remote(src, dst, send_sem, recv_sem, to):
         return pltpu.make_async_remote_copy(
@@ -192,7 +192,7 @@
         )
 
     def ask_line(d, axis, sign):
-        return remote(code, codes.at[pl.ds(d, 1), :], ds_sem.at[1], dr_sem.at[1], (axis, sign))
+        return remote(code, codes.at[d], ds_sem.at[1], dr_sem.at[1], (axis, sign))
 
     def ask_pairs(d, axis, sign):
         return remote(req, reqs.at[d], ds_sem.at[0], dr_sem.at[2], (axis, sign))
@@ -256,14 +256,12 @@
     for copy in inputs[2:4]:
         copy.wait()
     cols[0] = column(line_ref)
-    cols[1] = column(farline_ref)
-
-    codes[len(dirs) :] = jnp.zeros((8 - len(dirs), 128), f32)
+
     for d, (axis, sign) in enumerate(dirs):
 
         @pl.when(jnp.logical_not(exists(axis, -sign)))
         def _():
-            codes[pl.ds(d, 1), :] = jnp.zeros(code.shape, f32)
+            codes[d] = jnp.zeros(code.shape, f32)
             reqs[d] = jnp.zeros(req.shape, f32)
 
         @pl.when(jnp.logical_not(exists(axis, sign)))
@@ -362,11 +360,10 @@
     shifts = []
     for axis, sign in dirs:
         shifts.append([sign if a == axis else 0 for a in range(3)])
-    turned = jnp.transpose(codes[...])[outer:blocks]
     asked = []
     for d in range(len(dirs)):
-        there[d] = jnp.broadcast_to(turned[:, d : d + 1], (outer, pairs))
-        asked.append(located(there[d], 0.0, shifts[d])[0])
+        there = jnp.concatenate([codes[d]] * wide, axis=1)
+        asked.append(located(there, 0.0, shifts[d])[0])
     back = fetch(cat(asked))
     for d in range(len(dirs)):
         for c in range(3):
@@ -406,7 +403,8 @@
         got = [
             jnp.concatenate([reqs[d, c * wide + h] for h in range(wide)], axis=1) for c in range(4)
         ]
-        _, at, ok = located(there[d], got[3], shifts[d])
+        there = jnp.concatenate([codes[d]] * wide, axis=1)
+        _, at, ok = located(there, got[3], shifts[d])
         pairs_in.append([jnp.where(ok, at, 0.0)] + [jnp.where(ok, -got[c], 0.0) for c in range(3)])
     pairs_in = [cat([x[i] for x in pairs_in]) for i in range(4)]
     setup(0, cat(asked), pairs_in[0], pairs_in[1:])
@@ -611,9 +609,8 @@
             pltpu.VMEM((blocks, 3 * blk[2]), f32),
             pltpu.VMEM(positions.shape, f32),
             pltpu.VMEM((3, 3, blk[0] * blk[1], blk[2]), bf16),
-            pltpu.VMEM((1, 128), f32),
-            pltpu.VMEM((8, 128), f32),
-            pltpu.VMEM((6, outer, pairs), f32),
+            pltpu.VMEM((outer, 128), f32),
+            pltpu.VMEM((6, outer, 128), f32),
             pltpu.VMEM((6, 3, outer, blk[2]), f32),
             pltpu.VMEM((6, 3, outer, blk[2]), f32),
             pltpu.VMEM((4 * (pairs // 128), outer, 128), f32),

time: 38 us -> 38 us (level)
  no operation moved by 1% of the time
where the time goes in v7:
time: 38 us; the launch traced here: 37.9 us
  Pallas kernels  36.5 us (96%)
  between operations  1.31 us (3%)
    pallas_call x1, Pallas kernels, local(): pl.pallas_call(functools.partial(kernel, sizes, blk), out_shape=(pltpu.VM...  35.6 us
    pallas_call x1, Pallas kernels, local(): pl.pallas_call(finish, out_shape=(jax.ShapeDtypeStruct(positions.shape, f...  0.9 us

profile of v7, /device:TPU:0, one launch (start us, length us, event | category | flops | bytes accessed | tf_op | source)
XLA Modules:
  0.0 37.9 jit_solution(4338522728382679468)
XLA Ops:
  0.6 0.0 copy-start
  1.3 0.0 copy-done
  1.3 35.6 %shard_map.86 = (f32[3,16,16,256]{3,2,1,0:T(8,128)S(1)}, f32[2,5]{1,0:T(2,128)S(1)}) custom-call(s32[1,1,1]{2,1,0:T(1,128)S(6)} %copy.9.live_ref, s32[1,1,1,32,256]{4,3,2,1,0:T(8,128)} %node_hbm.1, s32[1,1,1,32]{3,2,1,0:T(1,128)} %line_hbm.1, s32[1,1,1,32,256]{4,3,2,1,0:T(8,128)} %farpos_hbm.1, s32[1,1,1,32]{3,2,1,0:T(1,128)S(1)} %copy-done, ...), custom_call_target="tpu_custom_call" | custom-call | tf_op jit(solution)/shard_map/pallas_call | solution.py:591
  37.0 0.9 %shard_map.87 = (f32[3,16,16,256]{3,2,1,0:T(8,128)}, f32[2,5]{1,0:T(2,128)}) custom-call(f32[3,16,16,256]{3,2,1,0:T(8,128)S(1)} %get-tuple-element.4.pos_ref, f32[2,5]{1,0:T(2,128)S(1)} %get-tuple-element.5.hist_ref), custom_call_target="tpu_custom_call" | custom-call | tf_op jit(solution)/shard_map/pallas_call | solution.py:652
Async XLA Ops:
  0.6 0.7 %copy-start = (s32[1,1,1,32]{3,2,1,0:T(1,128)S(1)}, s32[1,1,1,32]{3,2,1,0:T(1,128)}, u32[]{:S(2)}) copy-start(s32[1,1,1,32]{3,2,1,0:T(1,128)} %farline_ref.1) | copy-start | bytes 388

commit v8 on v7

--- a/solution.py
+++ b/solution.py
@@ -308,7 +308,7 @@
     def cat(parts, axis=0):
         return jnp.concatenate(parts, axis=axis)
 
-    def scatter(values):
+    def scatter(values, then=None):
         n = len(values)
         for h in range(bz // 128):
             for c in range(n):
@@ -316,6 +316,8 @@
                 for j in range(wide):
                     cut = x[:, 128 * j : 128 * (j + 1)]
                     terms[j, pl.ds(h * n + c, blocks, stride=group), :] = cut
+        if then is not None:
+            then()
         for b in range(blocks):
             slot = cat([terms[j, pl.ds(b * group, group), :] for j in range(wide)], 1)
             both = cat(split(slot, 2))
@@ -509,8 +511,12 @@
         last, slot = t == SWEEPS - 1, t % 2
         depth = jnp.where(live_rows, jnp.maximum(-gap[...], 0.0), 0.0)
         erecv[t, mine] = lanes_sum(depth * depth)
-        to_all(erecv.at[t, mine], es_sem.at[slot], er_sem.at[slot])
-        own = scatter([depth * geo[c, base : base + blocks] for c in range(3)])
+        send = functools.partial(to_all, erecv.at[t, mine], es_sem.at[slot], er_sem.at[slot])
+        if not last:
+            send()
+        own = scatter(
+            [depth * geo[c, base : base + blocks] for c in range(3)], send if last else None
+        )
         parts = cat(split(cat(own, 1), 2))
         if not t:
             wait_each(lrecv, ds_sem.at[1])

time: 38 us -> 38 us (level)
  no operation moved by 1% of the time
where the time goes in v8:
time: 38 us; the launch traced here: 37.9 us
  Pallas kernels  36.6 us (96%)
  between operations  1.31 us (3%)
    pallas_call x1, Pallas kernels, local(): pl.pallas_call(functools.partial(kernel, sizes, blk), out_shape=(pltpu.VM...  35.7 us
    pallas_call x1, Pallas kernels, local(): pl.pallas_call(finish, out_shape=(jax.ShapeDtypeStruct(positions.shape, f...  0.9 us

profile of v8, /device:TPU:0, one launch (start us, length us, event | category | flops | bytes accessed | tf_op | source)
XLA Modules:
  0.0 37.9 jit_solution(8509841727936143258)
XLA Ops:
  0.6 0.0 copy-start
  1.3 0.0 copy-done
  1.3 35.7 %shard_map.86 = (f32[3,16,16,256]{3,2,1,0:T(8,128)S(1)}, f32[2,5]{1,0:T(2,128)S(1)}) custom-call(s32[1,1,1]{2,1,0:T(1,128)S(6)} %copy.9.live_ref, s32[1,1,1,32,256]{4,3,2,1,0:T(8,128)} %node_hbm.1, s32[1,1,1,32]{3,2,1,0:T(1,128)} %line_hbm.1, s32[1,1,1,32,256]{4,3,2,1,0:T(8,128)} %farpos_hbm.1, s32[1,1,1,32]{3,2,1,0:T(1,128)S(1)} %copy-done, ...), custom_call_target="tpu_custom_call" | custom-call | tf_op jit(solution)/shard_map/pallas_call | solution.py:597
  37.0 0.9 %shard_map.87 = (f32[3,16,16,256]{3,2,1,0:T(8,128)}, f32[2,5]{1,0:T(2,128)}) custom-call(f32[3,16,16,256]{3,2,1,0:T(8,128)S(1)} %get-tuple-element.4.pos_ref, f32[2,5]{1,0:T(2,128)S(1)} %get-tuple-element.5.hist_ref), custom_call_target="tpu_custom_call" | custom-call | tf_op jit(solution)/shard_map/pallas_call | solution.py:658
Async XLA Ops:
  0.6 0.7 %copy-start = (s32[1,1,1,32]{3,2,1,0:T(1,128)S(1)}, s32[1,1,1,32]{3,2,1,0:T(1,128)}, u32[]{:S(2)}) copy-start(s32[1,1,1,32]{3,2,1,0:T(1,128)} %farline_ref.1) | copy-start | bytes 388
